TPU v7x, 512 devices: a whole 4x8x8 slice. The times are simulated.
512 devices in a mesh: dp: 32 (over y_lo, z), owner: 16 (over x, y_hi, core).
Axes of the slice: x: 4, y: 8 (y_hi: 2, y_lo: 4; y = y_hi * 4 + y_lo), z: 8, core: 2. Of those that a mesh axis runs over, the one named last changes fastest.
Arguments:
- gradients: bfloat16 [32, 16, 512, 512], P('dp', 'owner'), may hold values from -600 to 600
- block_layer: int32 [16], P('owner'), may hold values from 0 to 3
Outputs:
- update: bfloat16 [16, 512, 512], P('owner', 'dp')
All inputs are finite; a program needn't handle non-finite values.
Results may differ from a plain program's by a relative error of at most 0.0062.
Values may be sent and summed in bfloat16 or wider, within the bound.
No kernel may reach another device: no remote copies, remote signals or barrier semaphores. Data moves between devices by JAX's collectives and lax.ppermute only.
A program may use at most 64 MiB of HBM per device.

v0:
```python
import jax
import jax.numpy as jnp
from jax import lax
from jax.sharding import Mesh
from jax.sharding import PartitionSpec as P

LAYERS = 4
ITERS = 3
DP = ("dp_0", "dp_1")
DP_OWNER = ("dp_0", "dp_1", "owner_0", "owner_1", "owner_2")
OWNER = ("owner_0", "owner_1", "owner_2")


def from_partner(x, axis, distance):
    return lax.ppermute(x, axis, [(i, i ^ 1 << distance) for i in range(lax.axis_size(axis))])


def cut_along(x, dim, size):
    lengths = x.shape
    parts = x.reshape(*lengths[:dim], size, lengths[dim] // size, *lengths[dim + 1 :])
    return jnp.moveaxis(parts, dim, 0)


def summed_on_arrival(x, axis, dim):
    parts = cut_along(x, dim, lax.axis_size(axis))
    arrived = lax.all_to_all(parts, axis, split_axis=0, concat_axis=0, tiled=True)
    return arrived.sum(axis=0)


def sent_to_all(x, axis):
    size = lax.axis_size(axis)
    return lax.all_to_all(jnp.broadcast_to(x[None], (size, *x.shape)), axis, 0, 0, tiled=True)


def laid_out(parts, dim):
    lengths = list(parts.shape[1:])
    lengths[dim] *= parts.shape[0]
    return jnp.moveaxis(parts, 0, dim).reshape(lengths)


def gathered_copies(x, axis, dim):
    parts = sent_to_all(x, axis)
    return laid_out(parts, dim)


def by_axis(x, axes):
    for axis in axes:
        x = lax.psum(x, axis)
    return x


def own_whole(partial_rows, position, members):
    gathered = partial_rows
    for bit_number in range(members.bit_length() - 1):
        partner = from_partner(gathered, DP, bit_number)
        upper_half = position // (1 << bit_number) % 2 == 1
        gathered = jnp.where(
            upper_half,
            jnp.concatenate([partner, gathered], axis=0),
            jnp.concatenate([gathered, partner], axis=0),
        )
    return gathered


def keep_whole(partial_rows):
    return partial_rows


def root_slab(stat_rows, eye_rows, assemble):
    size_b = stat_rows.shape[1]
    identity = jnp.eye(size_b, dtype=jnp.float32)
    statistic = assemble(stat_rows)
    ridge_term = 0.01 * jnp.trace(statistic) / size_b + 1e-06
    shifted_whole = statistic + ridge_term * identity
    scaling = jnp.sqrt(jnp.sum(shifted_whole * shifted_whole))
    current_whole = shifted_whole / scaling
    current_rows = (stat_rows + ridge_term * eye_rows) / scaling
    inverse_rows = eye_rows
    for step_number in range(ITERS):
        factor_whole = (5.0 * identity - current_whole) / 4.0
        factor_rows = (5.0 * eye_rows - current_rows) / 4.0
        if step_number == 0:
            inverse_rows = scaling ** (-0.25) * factor_rows
        else:
            inverse_rows = jnp.dot(inverse_rows, factor_whole, precision=lax.Precision.HIGHEST)
        if step_number + 1 < ITERS:
            square_rows = jnp.dot(factor_rows, factor_whole, precision=lax.Precision.HIGHEST)
            square_whole = assemble(square_rows)
            fourth_rows = jnp.dot(square_rows, square_whole, precision=lax.Precision.HIGHEST)
            current_rows = jnp.dot(fourth_rows, current_whole, precision=lax.Precision.HIGHEST)
            current_whole = assemble(current_rows)
    return inverse_rows


def per_device(gradients, block_layer):
    gradient = gradients[0, 0]
    size_b = gradient.shape[0]
    dp_count = lax.axis_size(DP)
    members = dp_count // 2
    height = size_b // members
    position = lax.axis_index(DP)
    offset = position % members * height
    left_gram = lax.dot_general(
        gradient, gradient, (((1,), (1,)), ((), ())), preferred_element_type=jnp.float32
    )
    right_gram = lax.dot_general(
        gradient, gradient, (((0,), (0,)), ((), ())), preferred_element_type=jnp.float32
    )
    stacked = jnp.concatenate([left_gram, right_gram], axis=0)
    half_rows = summed_on_arrival(stacked, DP, 0)
    statistic = own_whole(half_rows, position, members)
    inverse_whole = root_slab(statistic, jnp.eye(size_b, dtype=jnp.float32), keep_whole)
    inverse_rows = lax.dynamic_slice_in_dim(inverse_whole, offset, height, 0)
    both_roots = gathered_copies(inverse_rows.astype(jnp.bfloat16), DP, 0)
    left_root = both_roots[:size_b]
    right_root = both_roots[size_b:]
    out_height = size_b // dp_count
    right_wide = right_root.astype(jnp.float32)
    left_part = lax.slice_in_dim(left_root, 0, out_height * lax.axis_size(DP), axis=0)
    middle = jnp.dot(left_part, gradient, preferred_element_type=jnp.float32)
    summed = summed_on_arrival(jnp.dot(middle, right_wide, precision=lax.Precision.HIGHEST), DP, 0)
    precond = summed / dp_count
    layer_id = block_layer[0]
    selector = (jnp.arange(LAYERS, dtype=jnp.int32) == layer_id).astype(jnp.float32)
    energy = jnp.sum(precond * precond)
    totals_sq, counts = (
        by_axis(selector * energy, DP_OWNER),
        by_axis(selector * float(precond.size), DP_OWNER),
    )
    mean_square = jnp.sum(selector * totals_sq) / jnp.sum(selector * counts)
    update = (precond * lax.rsqrt(mean_square + 1e-06)).astype(jnp.bfloat16)
    return update[None]


def solution(mesh):
    finer = Mesh(
        mesh.devices.reshape(4, 8, 4, 2, 2), ("dp_0", "dp_1", "owner_0", "owner_1", "owner_2")
    )
    in_specs = (P(DP, OWNER, None, None), P(OWNER))
    out_specs = P(OWNER, DP, None)
    return jax.shard_map(
        per_device, mesh=finer, in_specs=in_specs, out_specs=out_specs, check_vma=False
    )
```

profile of v0, /device:TPU:1, one launch (start us, length us, event | category | flops | bytes accessed | tf_op | source)
XLA Modules:
  0.0 257.0 jit_solution(7543262102058566053)
XLA Ops:
  0.0 1.0 copy-done
  2.2 62.1 %all_to_all.15 = f32[32,32,512]{2,1,0:T(8,128)S(1)} all-to-all(f32[32,32,512]{2,1,0:T(8,128)S(1)} %bitcast.32), channel_id=1, replica_groups=mesh['dp_0'=4,'dp_1'=8,'owner_0'=4,'owner_1'=2,'owner_2'=2] {'dp_0','dp_1'}, dimensions={0} | all-to-all | bytes 4194304 | tf_op jit(solution)/shard_map/all_to_all | solution.py:26
  64.4 4.5 %collective-permute-start = (f32[32,512]{1,0:T(8,128)S(1)}, f32[32,512]{1,0:T(8,128)S(1)}, u32[]{:S(2)}, u32[]{:S(2)}) collective-permute-start(f32[32,512]{1,0:T(8,128)S(1)} %reduce_sum.64), channel_id=1, source_target_pairs={{0,16},{16,0},{32,48},{48,32},{64,80},{80,64},{96,112},{112,96},{1... | collective-permute-start | bytes 196616 | tf_op jit(solution)/shard_map/ppermute | solution.py:15
  68.9 1.6 collective-permute-done
  70.6 4.3 %collective-permute-start.1 = (f32[64,512]{1,0:T(8,128)S(1)}, f32[64,512]{1,0:T(8,128)S(1)}, u32[]{:S(2)}, u32[]{:S(2)}) collective-permute-start(f32[64,512]{1,0:T(8,128)S(1)} %maximum_select_fusion.3), channel_id=1, source_target_pairs={{0,32},{16,48},{32,0},{48,16},{64,96},{80,112},{96,64},{112,80},{1... | collective-permute-start | bytes 393224 | tf_op jit(solution)/shard_map/ppermute | solution.py:15
  74.9 3.7 %collective-permute-done.1 = f32[64,512]{1,0:T(8,128)S(1)} collective-permute-done((f32[64,512]{1,0:T(8,128)S(1)}, f32[64,512]{1,0:T(8,128)S(1)}, u32[]{:S(2)}, u32[]{:S(2)}) %collective-permute-start.1) | collective-permute-done | bytes 131104 | tf_op jit(solution)/shard_map/ppermute | solution.py:15
  78.7 5.4 %collective-permute-start.2 = (f32[128,512]{1,0:T(8,128)S(1)}, f32[128,512]{1,0:T(8,128)S(1)}, u32[]{:S(2)}, u32[]{:S(2)}) collective-permute-start(f32[128,512]{1,0:T(8,128)S(1)} %maximum_select_fusion.2), channel_id=1, source_target_pairs={{0,64},{16,80},{32,96},{48,112},{64,0},{80,16},{96,32},{112,48},{1... | collective-permute-start | bytes 786440 | tf_op jit(solution)/shard_map/ppermute | solution.py:15
  84.1 12.8 %collective-permute-done.2 = f32[128,512]{1,0:T(8,128)S(1)} collective-permute-done((f32[128,512]{1,0:T(8,128)S(1)}, f32[128,512]{1,0:T(8,128)S(1)}, u32[]{:S(2)}, u32[]{:S(2)}) %collective-permute-start.2) | collective-permute-done | bytes 262176 | tf_op jit(solution)/shard_map/ppermute | solution.py:15
  96.9 1.9 collective-permute-start.3
  98.9 11.8 %collective-permute-done.3 = f32[256,512]{1,0:T(8,128)S(1)} collective-permute-done((f32[256,512]{1,0:T(8,128)S(1)}, f32[256,512]{1,0:T(8,128)S(1)}, u32[]{:S(2)}, u32[]{:S(2)}) %collective-permute-start.3) | collective-permute-done | bytes 524320 | tf_op jit(solution)/shard_map/ppermute | solution.py:15
  110.7 0.7 select_reduce_fusion
  112.0 0.9 multiply_reduce_fusion
  113.6 2.1 fusion.2
  115.7 2.8 %fusion.43 = f32[512,512]{1,0:T(8,128)} fusion(f32[512,512]{1,0:T(8,128)S(1)} %fusion.2), kind=kOutput, calls=%fused_computation.56 | convolution fusion | flops 1610612736 | bytes 2097152 | tf_op jit(solution)/shard_map/dot_general | solution.py:89
  118.6 3.2 %fusion.39 = f32[512,512]{1,0:T(8,128)S(1)} fusion(f32[512,512]{1,0:T(8,128)} %fusion.43, f32[]{:T(128)S(6)} %sqrt.3, f32[]{:T(128)S(6)} %add.61, f32[256,512]{1,0:T(8,128)S(1)} %collective-permute-done.3, f32[256,512]{1,0:T(8,128)S(1)} %maximum_select_fusion.1, pred[]{:T(512)S(6)} %eq.39), kind=kOutput, calls=%fused_computation.54 | convolution fusion | flops 1612447744 | bytes 3145737 | tf_op jit(solution)/shard_map/dot_general | solution.py:90
  121.8 1.9 fusion.7
  123.7 1.8 fusion.44
  125.5 1.9 fusion
  127.4 3.3 %fusion.4 = f32[512,512]{1,0:T(8,128)S(1)} fusion(f32[512,512]{1,0:T(8,128)S(1)} %fusion.39, f32[]{:T(128)S(6)} %mul.75, f32[]{:T(128)S(6)} %sqrt.3, f32[]{:T(128)S(6)} %add.61, f32[256,512]{1,0:T(8,128)} %copy-done.1, f32[256,512]{1,0:T(8,128)S(1)} %maximum_select_fusion.1, pred[]{:T(512)S(6)} %eq.39), kind=kOutput, calls=%fused_computation.9 | convolution fusion | flops 1614282752 | bytes 3145741 | tf_op jit(solution)/shard_map/dot_general | solution.py:85
  130.7 2.0 fusion.45
  132.9 32.6 %all_to_all.16 = bf16[32,32,512]{2,1,0:T(8,128)(2,1)S(1)} all-to-all(bf16[32,32,512]{2,1,0:T(8,128)(2,1)S(1)} %broadcast_in_dim.4), channel_id=1, replica_groups=mesh['dp_0'=4,'dp_1'=8,'owner_0'=4,'owner_1'=2,'owner_2'=2] {'dp_0','dp_1'}, dimensions={0} | all-to-all | bytes 2097152 | tf_op jit(solution)/shard_map/all_to_all | solution.py:32
  166.0 2.0 fusion.46
  168.0 8.0 %all-to-all-start.2 = ((f32[32,16,512]{2,1,0:T(8,128)}), f32[32,16,512]{2,1,0:T(8,128)S(1)}, u32[]{:S(2)}, u32[]{:S(2)}) async-start(f32[32,16,512]{2,1,0:T(8,128)} %fusion.46), calls=%async_computation.2 | async-start | bytes 2097152 | tf_op jit(solution)/shard_map/all_to_all | solution.py:26
  176.6 25.2 %all-to-all-done.2 = f32[32,16,512]{2,1,0:T(8,128)S(1)} async-done(((f32[32,16,512]{2,1,0:T(8,128)}), f32[32,16,512]{2,1,0:T(8,128)S(1)}, u32[]{:S(2)}, u32[]{:S(2)}) %all-to-all-start.2) | async-done | bytes 1048608 | tf_op jit(solution)/shard_map/all_to_all | solution.py:26
  202.5 0.6 fusion.28
  203.1 10.3 %all-reduce.2 = (f32[4]{0:T(128)S(1)}, f32[4]{0:T(128)S(1)}) all-reduce(f32[4]{0:T(128)S(1)} %fusion.28, f32[4]{0:T(128)S(1)} %fusion.27), channel_id=1, replica_groups=mesh['dp_0'=4,'dp_1'=8,'owner_0'=4,'owner_1'=2,'owner_2'=2] {'dp_0'}, use_global_device_ids=true, to_apply=%region_5.6 | all-reduce | flops 8 | bytes 64 | tf_op jit(solution)/shard_map/psum | solution.py:48
  213.4 13.0 %all-reduce = (f32[4]{0:T(128)S(1)}, f32[4]{0:T(128)S(1)}) all-reduce(f32[4]{0:T(128)S(1)} %get-tuple-element.9, f32[4]{0:T(128)S(1)} %get-tuple-element.10), channel_id=1, replica_groups=mesh['dp_0'=4,'dp_1'=8,'owner_0'=4,'owner_1'=2,'owner_2'=2] {'dp_1'}, use_global_device_ids=true, to_apply=%region_6.7 | all-reduce | flops 8 | bytes 64 | tf_op jit(solution)/shard_map/psum | solution.py:48
  226.4 8.9 %all-reduce.1 = (f32[4]{0:T(128)S(1)}, f32[4]{0:T(128)S(1)}) all-reduce(f32[4]{0:T(128)S(1)} %get-tuple-element.5, f32[4]{0:T(128)S(1)} %get-tuple-element.6), channel_id=1, replica_groups=mesh['dp_0'=4,'dp_1'=8,'owner_0'=4,'owner_1'=2,'owner_2'=2] {'owner_0'}, use_global_device_ids=true, to_apply=%region_7.8 | all-reduce | flops 8 | bytes 64 | tf_op jit(solution)/shard_map/psum | solution.py:48
  235.3 7.7 %all-reduce.4 = (f32[4]{0:T(128)S(1)}, f32[4]{0:T(128)S(1)}) all-reduce(f32[4]{0:T(128)S(1)} %get-tuple-element.7, f32[4]{0:T(128)S(1)} %get-tuple-element.8), channel_id=1, replica_groups=mesh['dp_0'=4,'dp_1'=8,'owner_0'=4,'owner_1'=2,'owner_2'=2] {'owner_1'}, use_global_device_ids=true, to_apply=%region_8.9 | all-reduce | flops 8 | bytes 64 | tf_op jit(solution)/shard_map/psum | solution.py:48
  243.0 11.3 %all-reduce.3 = (f32[4]{0:T(128)S(1)}, f32[4]{0:T(128)S(1)}) all-reduce(f32[4]{0:T(128)S(1)} %get-tuple-element.13, f32[4]{0:T(128)S(1)} %get-tuple-element.14), channel_id=1, replica_groups=mesh['dp_0'=4,'dp_1'=8,'owner_0'=4,'owner_1'=2,'owner_2'=2] {'owner_2'}, use_global_device_ids=true, to_apply=%region_9.10 | all-reduce | flops 8 | bytes 64 | tf_op jit(solution)/shard_map/psum | solution.py:48
  254.3 0.7 select_reduce_fusion.1
  256.4 0.6 fusion.26
  (17 shorter events, 2.7 us)
Async XLA Ops:
  0.0 1.0 copy-start
  64.4 6.1 %collective-permute-start = (f32[32,512]{1,0:T(8,128)S(1)}, f32[32,512]{1,0:T(8,128)S(1)}, u32[]{:S(2)}, u32[]{:S(2)}) collective-permute-start(f32[32,512]{1,0:T(8,128)S(1)} %reduce_sum.64), channel_id=1, source_target_pairs={{0,16},{16,0},{32,48},{48,32},{64,80},{80,64},{96,112},{112,96},{1... | collective-permute-start | bytes 196616 | tf_op jit(solution)/shard_map/ppermute | solution.py:15
  70.6 8.1 %collective-permute-start.1 = (f32[64,512]{1,0:T(8,128)S(1)}, f32[64,512]{1,0:T(8,128)S(1)}, u32[]{:S(2)}, u32[]{:S(2)}) collective-permute-start(f32[64,512]{1,0:T(8,128)S(1)} %maximum_select_fusion.3), channel_id=1, source_target_pairs={{0,32},{16,48},{32,0},{48,16},{64,96},{80,112},{96,64},{112,80},{1... | collective-permute-start | bytes 393224 | tf_op jit(solution)/shard_map/ppermute | solution.py:15
  78.7 18.2 %collective-permute-start.2 = (f32[128,512]{1,0:T(8,128)S(1)}, f32[128,512]{1,0:T(8,128)S(1)}, u32[]{:S(2)}, u32[]{:S(2)}) collective-permute-start(f32[128,512]{1,0:T(8,128)S(1)} %maximum_select_fusion.2), channel_id=1, source_target_pairs={{0,64},{16,80},{32,96},{48,112},{64,0},{80,16},{96,32},{112,48},{1... | collective-permute-start | bytes 786440 | tf_op jit(solution)/shard_map/ppermute | solution.py:15
  96.9 13.8 %collective-permute-start.3 = (f32[256,512]{1,0:T(8,128)S(1)}, f32[256,512]{1,0:T(8,128)S(1)}, u32[]{:S(2)}, u32[]{:S(2)}) collective-permute-start(f32[256,512]{1,0:T(8,128)S(1)} %maximum_select_fusion.1), channel_id=1, source_target_pairs={{0,128},{16,144},{32,160},{48,176},{64,192},{80,208},{96,224},{112... | collective-permute-start | bytes 1572872 | tf_op jit(solution)/shard_map/ppermute | solution.py:15
  110.7 7.9 %copy-start.1 = (f32[256,512]{1,0:T(8,128)}, f32[256,512]{1,0:T(8,128)S(1)}, u32[]{:S(2)}) copy-start(f32[256,512]{1,0:T(8,128)S(1)} %collective-permute-done.3) | copy-start | bytes 1572868
  168.0 33.8 %all-to-all-start.2 = ((f32[32,16,512]{2,1,0:T(8,128)}), f32[32,16,512]{2,1,0:T(8,128)S(1)}, u32[]{:S(2)}, u32[]{:S(2)}) async-start(f32[32,16,512]{2,1,0:T(8,128)} %fusion.46), calls=%async_computation.2 | async-start | bytes 2097152 | tf_op jit(solution)/shard_map/all_to_all | solution.py:26
where the time goes:
time: 258 us; the launch traced here: 257 us
  blocking collectives  146 us (57%)
  waiting for transfers between devices  55.1 us (21%)
  starting transfers between devices  24.1 us (9%)
  matrix products  22.3 us (9%)
  other arithmetic  4.59 us (2%)
  between operations  3.79 us (1%)
    all_to_all x1, blocking collectives, summed_on_arrival(): lax.all_to_all(parts, axis, split_axis=0, concat_axis=0, tiled=True)  62.1 us
    psum x5, blocking collectives, by_axis(): x = lax.psum(x, axis)  51.1 us
    all_to_all x1, blocking collectives, sent_to_all(): lax.all_to_all(jnp.broadcast_to(x[None], (size, *x.shape)), axis, 0, 0, t...  32.6 us
    ppermute x4, waiting for transfers between devices, from_partner(): lax.ppermute(x, axis, [(i, i ^ 1 << distance) for i in range(lax.axis_siz...  29.9 us
    all_to_all x1, waiting for transfers between devices, summed_on_arrival(): lax.all_to_all(parts, axis, split_axis=0, concat_axis=0, tiled=True)  25.2 us
    ppermute x4, starting transfers between devices, from_partner(): lax.ppermute(x, axis, [(i, i ^ 1 << distance) for i in range(lax.axis_siz...  16.1 us
    all_to_all x1, starting transfers between devices, summed_on_arrival(): lax.all_to_all(parts, axis, split_axis=0, concat_axis=0, tiled=True)  7.95 us
    dot_general x2, matrix products, root_slab(): jnp.dot(inverse_rows, factor_whole, precision=lax.Precision.HIGHEST)  5.3 us
  transfers between devices with their start and end apart: 5, of which 5 were waited for; matrix products, arithmetic and copies ran while one was open for 0% of the time, Pallas kernels for 0%

commit v1 on v0

v1 whole, which is shorter than its diff:
```python
import jax
import jax.numpy as jnp
from jax import lax
from jax.experimental import pallas as pl
from jax.experimental.pallas import tpu as pltpu
from jax.sharding import Mesh
from jax.sharding import PartitionSpec as P

DP = ("dp_0", "dp_1")
OWNER = ("owner_0", "owner_1", "owner_2")
B = 512
H = B // 2
LANE = 128
N_DP = 32
N_OWNER = 16
ROWS = B // N_DP
COLS = B // LANE
BODY = ROWS * COLS
DIAG = 8


def dot(a, b, contract=((1,), (0,))):
    return lax.dot_general(a, b, (contract, ((), ())), preferred_element_type=jnp.float32)


def triangle():
    row = lax.broadcasted_iota(jnp.int32, (H, H), 0)
    col = lax.broadcasted_iota(jnp.int32, (H, H), 1)
    return row, col


def pack_kernel(grad_ref, out_ref):
    grad = grad_ref[...]
    row, col = triangle()
    diagonals = []
    for stat in range(2):
        if stat == 0:
            first, second, contract = grad[:H], grad[H:], ((1,), (1,))
        else:
            first, second, contract = grad[:, :H], grad[:, H:], ((0,), (0,))
        upper = dot(first, first, contract)
        cross = dot(first, second, contract)
        lower = dot(second, second, contract)
        folded = jnp.where(row <= col, upper, lower).astype(jnp.bfloat16)
        cross = cross.astype(jnp.bfloat16)
        diagonal = jnp.sum(jnp.where(row == col, lower, 0.0), axis=0, keepdims=True)
        diagonals += [diagonal[:, :LANE], diagonal[:, LANE:]]
        slots = pl.ds(stat * N_DP // 2, N_DP // 2)
        for c, part in enumerate((cross[:, :LANE], cross[:, LANE:], folded[:, :LANE], folded[:, LANE:])):
            out_ref[slots, c * ROWS : (c + 1) * ROWS, :] = part.reshape(N_DP // 2, ROWS, LANE)
    out_ref[:, BODY : BODY + DIAG, :] = jnp.zeros((N_DP, DIAG, LANE), jnp.bfloat16)
    extra = jnp.concatenate(diagonals + [jnp.zeros((DIAG - 4, LANE), jnp.float32)], axis=0)
    out_ref[0, BODY : BODY + DIAG, :] = extra.astype(jnp.bfloat16)
    for c in range(COLS):
        start = BODY + DIAG + c * ROWS
        out_ref[:, start : start + ROWS, :] = grad[:, c * LANE : (c + 1) * LANE].reshape(N_DP, ROWS, LANE)


def inverse_root(statistic_parts, row, col):
    upper, cross, lower = statistic_parts
    on_diagonal = row == col
    trace = jnp.sum(jnp.where(on_diagonal, upper + lower, 0.0))
    ridge = 0.01 * trace / B + 1e-06
    upper = jnp.where(on_diagonal, upper + ridge, upper)
    lower = jnp.where(on_diagonal, lower + ridge, lower)
    total = jnp.sum(upper * upper + 2.0 * (cross * cross) + lower * lower)
    total = jnp.broadcast_to(total, (1, LANE))
    inverse_scale = lax.rsqrt(total)[:, :1]
    root_scale = jnp.exp(jnp.log(total) * -0.125)[:, :1]
    current = jnp.concatenate(
        [jnp.concatenate([upper, cross], axis=1), jnp.concatenate([cross.T, lower], axis=1)], axis=0
    ) * inverse_scale

    def advance(m):
        mb = m.astype(jnp.bfloat16)
        u = dot(mb, mb) * 0.0625 - 0.625 * m
        ub = u.astype(jnp.bfloat16)
        v = dot(ub, ub) + 3.125 * u
        return mb, dot(v.astype(jnp.bfloat16), mb) + 2.44140625 * m

    mb, second = advance(current)
    sb, third = advance(second)
    y = dot(mb, sb) * 0.0625 - 0.3125 * (current + second)
    tb = third.astype(jnp.bfloat16)
    z = dot(y.astype(jnp.bfloat16), tb)
    rest = 1.25 * y - 0.390625 * third - 0.25 * z
    full_row = lax.broadcasted_iota(jnp.int32, (B, B), 0)
    full_col = lax.broadcasted_iota(jnp.int32, (B, B), 1)
    return (jnp.where(full_row == full_col, rest + 1.953125, rest) * root_scale).astype(jnp.bfloat16)


def roots_kernel(stat_ref, left_ref, right_ref):
    row, col = triangle()
    for stat, out_ref in enumerate((left_ref, right_ref)):
        slots = pl.ds(stat * N_DP // 2, N_DP // 2)
        parts = [
            stat_ref[slots, c * ROWS : (c + 1) * ROWS, :].reshape(H, LANE).astype(jnp.float32)
            for c in range(COLS)
        ]
        cross = jnp.concatenate(parts[:2], axis=1)
        folded = jnp.concatenate(parts[2:], axis=1)
        flipped = folded.T
        extra = stat_ref[0, BODY : BODY + DIAG, :].astype(jnp.float32)
        diagonal = jnp.concatenate([extra[2 * stat : 2 * stat + 1], extra[2 * stat + 1 : 2 * stat + 2]], axis=1)
        upper = jnp.where(row <= col, folded, flipped)
        lower = jnp.where(row > col, folded, flipped)
        lower = jnp.where(row == col, diagonal, lower)
        out_ref[...] = inverse_root((upper, cross, lower), row, col)


def apply_kernel(place_ref, layer_ref, total_ref, left_ref, right_ref, rows_ref, note_ref, whole_ref):
    right = right_ref[...]
    total = jnp.concatenate(
        [total_ref[:, c * ROWS : (c + 1) * ROWS, :].reshape(B, LANE) for c in range(COLS)], axis=1
    )
    middle = dot(left_ref[...], total)
    high = middle.astype(jnp.bfloat16)
    low = (middle - high.astype(jnp.float32)).astype(jnp.bfloat16)
    whole = (dot(high, right) + dot(low, right)) * (1.0 / N_DP)
    whole_ref[...] = whole
    energy = jnp.sum(whole * whole)
    lane = lax.broadcasted_iota(jnp.int32, note_ref.shape, 2)
    note_ref[...] = jnp.where(lane == 0, energy, layer_ref[0].astype(jnp.float32))
    rows_ref[...] = whole_ref[pl.ds(place_ref[0] * ROWS, ROWS), :]


def scale_kernel(layer_ref, notes_ref, rows_ref, out_ref):
    notes = notes_ref[...]
    mine = notes[:, 0, 1:2] == layer_ref[0].astype(jnp.float32)
    energy = jnp.sum(jnp.where(mine, notes[:, 0, 0:1], 0.0), axis=0, keepdims=True)
    count = jnp.sum(jnp.where(mine, float(B * B), 0.0), axis=0, keepdims=True)
    out_ref[...] = (rows_ref[...] * lax.rsqrt(energy / count + 1e-06)).astype(jnp.bfloat16)


VMEM = pl.BlockSpec(memory_space=pltpu.VMEM)
SMEM = pl.BlockSpec(memory_space=pltpu.SMEM)


def shape(dims, dtype):
    return jax.ShapeDtypeStruct(dims, dtype)


def to_all(x, axes, size):
    return lax.all_to_all(jnp.broadcast_to(x[None], (size, *x.shape)), axes, 0, 0, tiled=True)


def per_device(gradients, block_layer):
    packed = pl.pallas_call(
        pack_kernel,
        out_shape=shape((N_DP, 2 * BODY + DIAG, LANE), jnp.bfloat16),
        in_specs=[VMEM],
        out_specs=VMEM,
        name="pack",
    )(gradients[0, 0])
    arrived = lax.all_to_all(packed, DP, 0, 0, tiled=True)
    mine = jnp.sum(arrived.astype(jnp.float32), axis=0).astype(jnp.bfloat16)
    stats = to_all(mine[: BODY + DIAG], DP, N_DP)
    stats, total = lax.optimization_barrier((stats, mine[BODY + DIAG :]))
    total = to_all(total, DP, N_DP)
    left, right = pl.pallas_call(
        roots_kernel,
        out_shape=(shape((B, B), jnp.bfloat16), shape((B, B), jnp.bfloat16)),
        in_specs=[VMEM],
        out_specs=(VMEM, VMEM),
        cost_estimate=pl.CostEstimate(flops=10 * 16 * 2 * B**3, bytes_accessed=2 * B * B * 4, transcendentals=0),
        name="roots",
    )(stats)
    place = lax.axis_index(DP)[None].astype(jnp.int32)
    rows, note = pl.pallas_call(
        apply_kernel,
        out_shape=(shape((ROWS, B), jnp.float32), shape((N_OWNER, 1, LANE), jnp.float32)),
        in_specs=[SMEM, SMEM, VMEM, VMEM, VMEM],
        out_specs=(VMEM, VMEM),
        scratch_shapes=[pltpu.VMEM((B, B), jnp.float32)],
        name="apply",
    )(place, block_layer, total, left, right)
    notes = lax.all_to_all(note, OWNER, 0, 0, tiled=True)
    update = pl.pallas_call(
        scale_kernel,
        out_shape=shape((ROWS, B), jnp.bfloat16),
        in_specs=[SMEM, VMEM, VMEM],
        out_specs=VMEM,
        name="scale",
    )(block_layer, notes, rows)
    return update[None]


def solution(mesh):
    finer = Mesh(
        mesh.devices.reshape(4, 8, 4, 2, 2), ("dp_0", "dp_1", "owner_0", "owner_1", "owner_2")
    )
    in_specs = (P(DP, OWNER, None, None), P(OWNER))
    out_specs = P(OWNER, DP, None)
    return jax.shard_map(
        per_device, mesh=finer, in_specs=in_specs, out_specs=out_specs, check_vma=False
    )
```

time: 258 us -> 117 us (0.45)
  blocking collectives: 146 us -> 63.5 us
  waiting for transfers between devices: 55.1 us -> 22.1 us
  matrix products: 22.3 us -> 0 us
  Pallas kernels: 0 us -> 15.1 us
  starting transfers between devices: 24.1 us -> 12.4 us
  other arithmetic: 4.59 us -> 0.16 us
  between operations: 3.79 us -> 0.7 us
    psum x5 -> x0, blocking collectives: 51.1 us -> none  [by_axis(): x = lax.psum(x, axis)]
    all_to_all x2, blocking collectives: 94.7 us -> 63.5 us  [the longest x1 44.8 us: per_device(): arrived = lax.all_to_all(packed, DP, 0, 0, tiled=True)]
    ppermute x4 -> x0, waiting for transfers between devices: 29.9 us -> none  [from_partner(): lax.ppermute(x, axis, [(i, i ^ 1 << distance) for i in range(lax.axis_siz...]
    dot_general x12 -> x0, matrix products: 22.3 us -> none  [the longest x2 5.3 us: root_slab(): jnp.dot(inverse_rows, factor_whole, precision=lax.Precision.HIGHEST)]
    ppermute x4 -> x0, starting transfers between devices: 16.1 us -> none  [from_partner(): lax.ppermute(x, axis, [(i, i ^ 1 << distance) for i in range(lax.axis_siz...]
    pallas_call x0 -> x4, Pallas kernels: none -> 15.1 us  [the longest x1 7.69 us: per_device(): pl.pallas_call(roots_kernel, out_shape=(shape((B, B), jnp.bfloat16), shap...]
    all_to_all x1 -> x2, starting transfers between devices: 7.95 us -> 12.4 us  [to_all(): lax.all_to_all(jnp.broadcast_to(x[None], (size, *x.shape)), axes, 0, 0, t...]
    all_to_all x1 -> x2, waiting for transfers between devices: 25.2 us -> 22.1 us  [to_all(): lax.all_to_all(jnp.broadcast_to(x[None], (size, *x.shape)), axes, 0, 0, t...]
  transfers between devices with their start and end apart: 5 -> 2, of which waited for: 5 -> 2; matrix products, arithmetic and copies ran while one was open for 0% -> 0% of each run, Pallas kernels for 0% -> 7%
where the time goes in v1:
time: 117 us
  blocking collectives  63.5 us (54%)
  waiting for transfers between devices  22.1 us (19%)
  Pallas kernels  15.1 us (13%)
  starting transfers between devices  12.4 us (11%)
  local copies, waits for them, and re-layouts  2.69 us (2%)
    all_to_all x1, blocking collectives, per_device(): arrived = lax.all_to_all(packed, DP, 0, 0, tiled=True)  44.8 us
    all_to_all x2, waiting for transfers between devices, to_all(): lax.all_to_all(jnp.broadcast_to(x[None], (size, *x.shape)), axes, 0, 0, t...  22.1 us
    all_to_all x1, blocking collectives, per_device(): notes = lax.all_to_all(note, OWNER, 0, 0, tiled=True)  18.7 us
    all_to_all x2, starting transfers between devices, to_all(): lax.all_to_all(jnp.broadcast_to(x[None], (size, *x.shape)), axes, 0, 0, t...  12.4 us
    pallas_call x1, Pallas kernels, per_device(): pl.pallas_call(roots_kernel, out_shape=(shape((B, B), jnp.bfloat16), shap...  7.69 us
    pallas_call x1, Pallas kernels, per_device(): pl.pallas_call(apply_kernel, out_shape=(shape((ROWS, B), jnp.float32), sh...  3.2 us
    pallas_call x1, Pallas kernels, per_device(): pl.pallas_call(pack_kernel, out_shape=shape((N_DP, 2 * BODY + DIAG, LANE)...  2.69 us
  transfers between devices with their start and end apart: 2, of which 2 were waited for; matrix products, arithmetic and copies ran while one was open for 0% of the time, Pallas kernels for 7%

profile of v1, /device:TPU:1, one launch (start us, length us, event | category | flops | bytes accessed | tf_op | source)
XLA Modules:
  0.0 116.6 jit_solution(4291519015542479559)
XLA Ops:
  0.0 2.7 %pack.1 = bf16[32,136,128]{2,1,0:T(8,128)(2,1)} custom-call(bf16[512,512]{1,0:T(8,128)(2,1)} %bitcast.3), custom_call_target="tpu_custom_call" | custom-call | tf_op jit(solution)/shard_map/pack/pallas_call | solution.py:148
  2.7 44.8 %all_to_all.20 = bf16[32,136,128]{2,1,0:T(8,128)(2,1)S(1)} all-to-all(bf16[32,136,128]{2,1,0:T(8,128)(2,1)} %pack.1), channel_id=1, replica_groups=mesh['dp_0'=4,'dp_1'=8,'owner_0'=4,'owner_1'=2,'owner_2'=2] {'dp_0','dp_1'}, dimensions={0} | all-to-all | bytes 2228224 | tf_op jit(solution)/shard_map/all_to_all | solution.py:155
  47.5 0.2 reduce_sum.12
  47.6 0.9 broadcast_in_dim.9
  48.5 4.1 %all-to-all-start.1 = ((bf16[32,72,128]{2,1,0:T(8,128)(2,1)}), bf16[32,72,128]{2,1,0:T(8,128)(2,1)S(1)}, u32[]{:S(2)}, u32[]{:S(2)}) async-start(bf16[32,72,128]{2,1,0:T(8,128)(2,1)} %broadcast_in_dim.9), calls=%async_computation.1 | async-start | bytes 1179648 | tf_op jit(solution)/shard_map/all_to_all | solution.py:144
  53.4 14.7 %all-to-all-done.1.stat_ref = bf16[32,72,128]{2,1,0:T(8,128)(2,1)S(1)} async-done(((bf16[32,72,128]{2,1,0:T(8,128)(2,1)}), bf16[32,72,128]{2,1,0:T(8,128)(2,1)S(1)}, u32[]{:S(2)}, u32[]{:S(2)}) %all-to-all-start.1) | async-done | bytes 589856 | tf_op jit(solution)/shard_map/all_to_all | solution.py:144
  68.1 0.0 copy-start.1
  68.1 1.0 broadcast_in_dim.20
  69.1 8.3 %all-to-all-start.2 = ((bf16[32,64,128]{2,1,0:T(8,128)(2,1)}), bf16[32,64,128]{2,1,0:T(8,128)(2,1)S(1)}, u32[]{:S(2)}, u32[]{:S(2)}) async-start(bf16[32,64,128]{2,1,0:T(8,128)(2,1)} %broadcast_in_dim.20), calls=%async_computation.2 | async-start | bytes 1048576 | tf_op jit(solution)/shard_map/all_to_all | solution.py:144
  77.4 0.0 copy-done.1
  77.4 7.7 %roots.1 = (bf16[512,512]{1,0:T(8,128)(2,1)}, bf16[512,512]{1,0:T(8,128)(2,1)}) custom-call(bf16[32,72,128]{2,1,0:T(8,128)(2,1)} %copy-done.1), custom_call_target="tpu_custom_call" | custom-call | flops 42949672960 | bytes 2097152 | tf_op jit(solution)/shard_map/roots/pallas_call | solution.py:160
  85.1 7.3 %all-to-all-done.2.total_ref = bf16[32,64,128]{2,1,0:T(8,128)(2,1)S(1)} async-done(((bf16[32,64,128]{2,1,0:T(8,128)(2,1)}), bf16[32,64,128]{2,1,0:T(8,128)(2,1)S(1)}, u32[]{:S(2)}, u32[]{:S(2)}) %all-to-all-start.2) | async-done | bytes 524320 | tf_op jit(solution)/shard_map/all_to_all | solution.py:144
  92.4 0.0 copy-start
  92.4 0.8 copy-done
  93.2 3.2 %apply.1 = (f32[16,512]{1,0:T(8,128)}, f32[16,1,128]{2,1,0:T(1,128)}) custom-call(s32[1]{0:T(128)} %bitcast.place_ref, s32[1]{0:T(128)S(6)} %copy.3.layer_ref, bf16[32,64,128]{2,1,0:T(8,128)(2,1)} %copy-done, bf16[512,512]{1,0:T(8,128)(2,1)} %get-tuple-element.13.left_ref, bf16[512,512]{1,0:T(8,128)(2,1)} %get-tuple-element.14.right_ref), custom_call_target="tpu_custom_call" | custom-call | tf_op jit(solution)/shard_map/apply/pallas_call | solution.py:169
  96.4 18.7 %all_to_all.21.notes_ref = f32[16,1,128]{2,1,0:T(1,128)} all-to-all(f32[16,1,128]{2,1,0:T(1,128)} %get-tuple-element.15), channel_id=1, replica_groups=mesh['dp_0'=4,'dp_1'=8,'owner_0'=4,'owner_1'=2,'owner_2'=2] {'owner_0','..., dimensions={0} | all-to-all | bytes 16384 | tf_op jit(solution)/shard_map/all_to_all | solution.py:177
  115.1 1.6 %scale.1 = bf16[16,512]{1,0:T(8,128)(2,1)} custom-call(s32[1]{0:T(128)S(6)} %copy.3.layer_ref, f32[16,1,128]{2,1,0:T(1,128)} %all_to_all.21.notes_ref, f32[16,512]{1,0:T(8,128)} %get-tuple-element.16.rows_ref), custom_call_target="tpu_custom_call" | custom-call | tf_op jit(solution)/shard_map/scale/pallas_call | solution.py:178
  (2 shorter events, 0.0 us)
Async XLA Ops:
  48.5 19.5 %all-to-all-start.1 = ((bf16[32,72,128]{2,1,0:T(8,128)(2,1)}), bf16[32,72,128]{2,1,0:T(8,128)(2,1)S(1)}, u32[]{:S(2)}, u32[]{:S(2)}) async-start(bf16[32,72,128]{2,1,0:T(8,128)(2,1)} %broadcast_in_dim.9), calls=%async_computation.1 | async-start | bytes 1179648 | tf_op jit(solution)/shard_map/all_to_all | solution.py:144
  68.1 9.3 %copy-start.1 = (bf16[32,72,128]{2,1,0:T(8,128)(2,1)}, bf16[32,72,128]{2,1,0:T(8,128)(2,1)S(1)}, u32[]{:S(2)}) copy-start(bf16[32,72,128]{2,1,0:T(8,128)(2,1)S(1)} %all-to-all-done.1.stat_ref) | copy-start | bytes 1769476
  69.1 23.3 %all-to-all-start.2 = ((bf16[32,64,128]{2,1,0:T(8,128)(2,1)}), bf16[32,64,128]{2,1,0:T(8,128)(2,1)S(1)}, u32[]{:S(2)}, u32[]{:S(2)}) async-start(bf16[32,64,128]{2,1,0:T(8,128)(2,1)} %broadcast_in_dim.20), calls=%async_computation.2 | async-start | bytes 1048576 | tf_op jit(solution)/shard_map/all_to_all | solution.py:144
  92.4 0.8 copy-start

commit v2 on v1

v2 whole, which is shorter than its diff:
```python
import jax
import jax.numpy as jnp
from jax import lax
from jax.experimental import pallas as pl
from jax.experimental.pallas import tpu as pltpu
from jax.sharding import Mesh
from jax.sharding import PartitionSpec as P

DP = ("q", "p", "z")
OWNER = ("x", "h", "c")
PEERS = ("q", "z")
CHIP_PAIR = ("p", "c")
NOTE_AXES = ("q", "p", "x", "h", "c")
B = 512
H = B // 2
LANE = 128
N_DP = 32
N_PEER = 16
N_NOTE = 32
ROWS = B // N_DP
SLAB = H // N_PEER
COLS = B // LANE
BODY = SLAB * COLS
DIAG = 8


def dot(a, b, contract=((1,), (0,))):
    return lax.dot_general(a, b, (contract, ((), ())), preferred_element_type=jnp.float32)


def triangle():
    row = lax.broadcasted_iota(jnp.int32, (H, H), 0)
    col = lax.broadcasted_iota(jnp.int32, (H, H), 1)
    return row, col


def pack_kernel(role_ref, one_ref, two_ref, out_ref):
    row, col = triangle()

    def pack(role):
        upper = cross = lower = 0.0
        for ref in (one_ref, two_ref):
            if role == 0:
                first, second, contract = ref[:H], ref[H:], ((1,), (1,))
            else:
                first, second, contract = ref[:, :H], ref[:, H:], ((0,), (0,))
            upper += dot(first, first, contract)
            cross += dot(first, second, contract)
            lower += dot(second, second, contract)
        folded = jnp.where(row <= col, upper, lower).astype(jnp.bfloat16)
        cross = cross.astype(jnp.bfloat16)
        diagonal = jnp.sum(jnp.where(row == col, lower, 0.0), axis=0, keepdims=True)
        for c, part in enumerate((cross[:, :LANE], cross[:, LANE:], folded[:, :LANE], folded[:, LANE:])):
            out_ref[:, c * SLAB : (c + 1) * SLAB, :] = part.reshape(N_PEER, SLAB, LANE)
        out_ref[:, BODY : BODY + DIAG, :] = jnp.zeros((N_PEER, DIAG, LANE), jnp.bfloat16)
        extra = jnp.concatenate(
            [diagonal[:, :LANE], diagonal[:, LANE:], jnp.zeros((DIAG - 2, LANE), jnp.float32)], axis=0
        )
        out_ref[0, BODY : BODY + DIAG, :] = extra.astype(jnp.bfloat16)
        half = slice(role * H, (role + 1) * H)
        total = (one_ref[half].astype(jnp.float32) + two_ref[half].astype(jnp.float32)).astype(jnp.bfloat16)
        for c in range(COLS):
            start = BODY + DIAG + c * SLAB
            out_ref[:, start : start + SLAB, :] = total[:, c * LANE : (c + 1) * LANE].reshape(N_PEER, SLAB, LANE)

    for role in range(2):
        pl.when(role_ref[0] == role)(lambda role=role: pack(role))


def inverse_root(statistic_parts, row, col):
    upper, cross, lower = statistic_parts
    on_diagonal = row == col
    trace = jnp.sum(jnp.where(on_diagonal, upper + lower, 0.0))
    ridge = 0.01 * trace / B + 1e-06
    upper = jnp.where(on_diagonal, upper + ridge, upper)
    lower = jnp.where(on_diagonal, lower + ridge, lower)
    total = jnp.sum(upper * upper + 2.0 * (cross * cross) + lower * lower)
    total = jnp.broadcast_to(total, (1, LANE))
    inverse_scale = lax.rsqrt(total)[:, :1]
    root_scale = jnp.exp(jnp.log(total) * -0.125)[:, :1]
    current = jnp.concatenate(
        [jnp.concatenate([upper, cross], axis=1), jnp.concatenate([cross.T, lower], axis=1)], axis=0
    ) * inverse_scale

    def advance(m):
        mb = m.astype(jnp.bfloat16)
        u = dot(mb, mb) * 0.0625 - 0.625 * m
        ub = u.astype(jnp.bfloat16)
        v = dot(ub, ub) + 3.125 * u
        return mb, dot(v.astype(jnp.bfloat16), mb) + 2.44140625 * m

    mb, second = advance(current)
    sb, third = advance(second)
    y = dot(mb, sb) * 0.0625 - 0.3125 * (current + second)
    tb = third.astype(jnp.bfloat16)
    z = dot(y.astype(jnp.bfloat16), tb)
    rest = 1.25 * y - 0.390625 * third - 0.25 * z
    full_row = lax.broadcasted_iota(jnp.int32, (B, B), 0)
    full_col = lax.broadcasted_iota(jnp.int32, (B, B), 1)
    return (jnp.where(full_row == full_col, rest + 1.953125, rest) * root_scale).astype(jnp.bfloat16)


def root_kernel(stat_ref, out_ref):
    row, col = triangle()
    parts = [
        stat_ref[:, c * SLAB : (c + 1) * SLAB, :].reshape(H, LANE).astype(jnp.float32)
        for c in range(COLS)
    ]
    cross = jnp.concatenate(parts[:2], axis=1)
    folded = jnp.concatenate(parts[2:], axis=1)
    flipped = folded.T
    extra = stat_ref[0, BODY : BODY + DIAG, :].astype(jnp.float32)
    diagonal = jnp.concatenate([extra[0:1], extra[1:2]], axis=1)
    upper = jnp.where(row <= col, folded, flipped)
    lower = jnp.where(row > col, folded, flipped)
    lower = jnp.where(row == col, diagonal, lower)
    out_ref[...] = inverse_root((upper, cross, lower), row, col)


def apply_kernel(scalar_ref, mine_ref, half_ref, root_ref, other_ref, rows_ref, note_ref, whole_ref):
    role = scalar_ref[0]
    start = BODY + DIAG

    def wide(ref, offset):
        return jnp.concatenate(
            [
                ref[:, offset + c * SLAB : offset + (c + 1) * SLAB, :].reshape(H, LANE)
                for c in range(COLS)
            ],
            axis=1,
        )

    def apply(left_ref, right_ref, top, bottom):
        right = right_ref[...]
        middle = dot(left_ref[:, :H], top) + dot(left_ref[:, H:], bottom)
        high = middle.astype(jnp.bfloat16)
        low = (middle - high.astype(jnp.float32)).astype(jnp.bfloat16)
        whole = (dot(high, right) + dot(low, right)) * (1.0 / N_DP)
        whole_ref[...] = whole
        energy = jnp.sum(whole * whole)
        lane = lax.broadcasted_iota(jnp.int32, note_ref.shape, 2)
        layer = scalar_ref[2].astype(jnp.float32)
        note_ref[...] = jnp.where(lane == 0, energy, layer)

    @pl.when(role == 0)
    def _():
        apply(root_ref, other_ref, wide(mine_ref, start), wide(half_ref, 0))

    @pl.when(role == 1)
    def _():
        apply(other_ref, root_ref, wide(half_ref, 0), wide(mine_ref, start))

    rows_ref[...] = whole_ref[pl.ds(scalar_ref[1] * ROWS, ROWS), :]


def scale_kernel(scalar_ref, notes_ref, rows_ref, moved_ref, out_ref):
    notes = notes_ref[...]
    mine = notes[:, 0, 1:2] == scalar_ref[0].astype(jnp.float32)
    energy = jnp.sum(jnp.where(mine, notes[:, 0, 0:1], 0.0), axis=0, keepdims=True)
    count = jnp.sum(jnp.where(mine, float(B * B), 0.0), axis=0, keepdims=True)
    rows = jnp.where(scalar_ref[1] == 1, rows_ref[...], moved_ref[...])
    out_ref[...] = (rows * lax.rsqrt(energy / count + 1e-06)).astype(jnp.bfloat16)


VMEM = pl.BlockSpec(memory_space=pltpu.VMEM)
SMEM = pl.BlockSpec(memory_space=pltpu.SMEM)


def near(x):
    return pltpu.with_memory_space_constraint(x, pltpu.VMEM)


def to_all(x, axes, size):
    return lax.all_to_all(jnp.broadcast_to(x[None], (size, *x.shape)), axes, 0, 0, tiled=True)


def note_groups():
    groups = []
    for q in range(2):
        groups.append(
            [
                (((q ^ h) * 2 + p) * 4 + x) * 4 + h * 2 + c
                for p in range(2)
                for x in range(4)
                for h in range(2)
                for c in range(2)
            ]
        )
    return groups


SWAP = [(1, 2), (2, 1)]
ACROSS = [(0, 1), (1, 0)]


def per_device(gradients, block_layer):
    own = gradients[0, 0]
    role = lax.axis_index("c")
    keeper = role == lax.axis_index("p")
    swapped = lax.ppermute(own, CHIP_PAIR, SWAP)
    one = jnp.where(keeper, own, swapped)
    two = lax.ppermute(one, "c", ACROSS)
    packed = pl.pallas_call(
        pack_kernel,
        out_shape=pltpu.VMEM((N_PEER, 2 * BODY + DIAG, LANE), jnp.bfloat16),
        in_specs=[SMEM, VMEM, VMEM],
        out_specs=VMEM,
        name="pack",
    )(role[None], near(one), near(two))
    arrived = lax.all_to_all(packed, PEERS, 0, 0, tiled=True)
    mine = jnp.sum(arrived.astype(jnp.float32), axis=0).astype(jnp.bfloat16)
    everything = to_all(mine, PEERS, N_PEER)
    half = lax.ppermute(everything[:, BODY + DIAG :], "c", ACROSS)
    root = pl.pallas_call(
        root_kernel,
        out_shape=pltpu.VMEM((B, B), jnp.bfloat16),
        in_specs=[VMEM],
        out_specs=VMEM,
        name="root",
    )(near(everything))
    other = lax.ppermute(root, "c", ACROSS)
    place = (lax.axis_index("q") * 2 + role) * 8 + lax.axis_index("z")
    layer = jnp.where(keeper, block_layer[0], -1)
    scalars = jnp.stack([role, place, layer]).astype(jnp.int32)
    rows, note = pl.pallas_call(
        apply_kernel,
        out_shape=(
            pltpu.VMEM((ROWS, B), jnp.float32),
            pltpu.VMEM((N_NOTE, 1, LANE), jnp.float32),
        ),
        in_specs=[SMEM, VMEM, VMEM, VMEM, VMEM],
        out_specs=(VMEM, VMEM),
        scratch_shapes=[pltpu.VMEM((B, B), jnp.float32)],
        name="apply",
    )(scalars, near(everything), near(half), near(root), near(other))
    moved = lax.ppermute(rows, CHIP_PAIR, SWAP)
    notes = lax.all_to_all(note, NOTE_AXES, 0, 0, tiled=True, axis_index_groups=note_groups())
    update = pl.pallas_call(
        scale_kernel,
        out_shape=jax.ShapeDtypeStruct((ROWS, B), jnp.bfloat16),
        in_specs=[SMEM, VMEM, VMEM, VMEM],
        out_specs=VMEM,
        name="scale",
    )(jnp.stack([block_layer[0], keeper.astype(jnp.int32)]), near(notes), near(rows), near(moved))
    return update[None]


def solution(mesh):
    finer = Mesh(mesh.devices.reshape(2, 2, 8, 4, 2, 2), DP + OWNER)
    in_specs = (P(DP, OWNER, None, None), P(OWNER))
    out_specs = P(OWNER, DP, None)
    return jax.shard_map(
        per_device, mesh=finer, in_specs=in_specs, out_specs=out_specs, check_vma=False
    )
```

time: 117 us -> 100 us (0.85)
  blocking collectives: 63.5 us -> 52.6 us
  starting transfers between devices: 12.4 us -> 22.8 us
  waiting for transfers between devices: 22.1 us -> 12.5 us
  Pallas kernels: 15.1 us -> 7.85 us
  local copies, waits for them, and re-layouts: 2.69 us -> 0.09 us
  other arithmetic: 0.16 us -> 2.4 us
    all_to_all x2 -> x1, waiting for transfers between devices: 22.1 us -> 3.36 us  [per_device(): lax.all_to_all(note, NOTE_AXES, 0, 0, tiled=True, axis_index_groups=note_...]
    ppermute x0 -> x5, starting transfers between devices: none -> 16.7 us  [the longest x1 4.72 us: per_device(): other = lax.ppermute(root, 'c', ACROSS)]
    all_to_all x2, blocking collectives: 63.5 us -> 52.6 us  [the longest x1 31.6 us: per_device(): arrived = lax.all_to_all(packed, PEERS, 0, 0, tiled=True)]
    ppermute x0 -> x5, waiting for transfers between devices: none -> 9.13 us  [the longest x1 7.05 us: per_device(): swapped = lax.ppermute(own, CHIP_PAIR, SWAP)]
    pallas_call x4, Pallas kernels: 15.1 us -> 7.85 us  [the longest x1 3.19 us: per_device(): pl.pallas_call(root_kernel, out_shape=pltpu.VMEM((B, B), jnp.bfloat16), i...]
    all_to_all x2 -> x1, starting transfers between devices: 12.4 us -> 6.09 us  [per_device(): lax.all_to_all(note, NOTE_AXES, 0, 0, tiled=True, axis_index_groups=note_...]
    broadcast_in_dim x2 -> x1, local copies, waits for them, and re-layouts: 1.89 us -> 0.07 us  [to_all(): jnp.broadcast_to(x[None], (size, *x.shape))]
    another operation x0 -> x2, other arithmetic: none -> 1.22 us  [the longest x1 0.64 us: per_device(): scalars = jnp.stack([role, place, layer]).astype(jnp.int32)]
  transfers between devices with their start and end apart: 2 -> 6, of which waited for: 2 -> 4; matrix products, arithmetic and copies ran while one was open for 0% -> 1% of each run, Pallas kernels for 7% -> 0%
where the time goes in v2:
time: 100 us; the launch traced here: 99 us
  blocking collectives  52.6 us (53%)
  starting transfers between devices  22.8 us (23%)
  waiting for transfers between devices  12.5 us (12%)
  Pallas kernels  7.85 us (8%)
  other arithmetic  2.4 us (2%)
    all_to_all x1, blocking collectives, per_device(): arrived = lax.all_to_all(packed, PEERS, 0, 0, tiled=True)  31.6 us
    all_to_all x1, blocking collectives, to_all(): lax.all_to_all(jnp.broadcast_to(x[None], (size, *x.shape)), axes, 0, 0, t...  21 us
    ppermute x1, waiting for transfers between devices, per_device(): swapped = lax.ppermute(own, CHIP_PAIR, SWAP)  7.05 us
    all_to_all x1, starting transfers between devices, per_device(): lax.all_to_all(note, NOTE_AXES, 0, 0, tiled=True, axis_index_groups=note_...  6.09 us
    ppermute x1, starting transfers between devices, per_device(): other = lax.ppermute(root, 'c', ACROSS)  4.72 us
    ppermute x1, starting transfers between devices, per_device(): swapped = lax.ppermute(own, CHIP_PAIR, SWAP)  4.57 us
    ppermute x1, starting transfers between devices, per_device(): moved = lax.ppermute(rows, CHIP_PAIR, SWAP)  3.55 us
    all_to_all x1, waiting for transfers between devices, per_device(): lax.all_to_all(note, NOTE_AXES, 0, 0, tiled=True, axis_index_groups=note_...  3.36 us
  transfers between devices with their start and end apart: 6, of which 4 were waited for; matrix products, arithmetic and copies ran while one was open for 1% of the time, Pallas kernels for 0%

profile of v2, /device:TPU:1, one launch (start us, length us, event | category | flops | bytes accessed | tf_op | source)
XLA Modules:
  0.0 99.0 jit_solution(2935067544555335508)
XLA Ops:
  0.0 4.6 %collective-permute-start = (bf16[512,512]{1,0:T(8,128)(2,1)}, bf16[512,512]{1,0:T(8,128)(2,1)S(1)}, u32[]{:S(2)}, u32[]{:S(2)}) collective-permute-start(bf16[512,512]{1,0:T(8,128)(2,1)} %bitcast.9), channel_id=1, source_target_pairs={{1,128},{128,1},{3,130},{130,3},{5,132},{132,5},{7,134},{134,7},{9... | collective-permute-start | bytes 1572872 | tf_op jit(solution)/shard_map/ppermute | solution.py:200
  4.6 7.1 %collective-permute-done = bf16[512,512]{1,0:T(8,128)(2,1)S(1)} collective-permute-done((bf16[512,512]{1,0:T(8,128)(2,1)}, bf16[512,512]{1,0:T(8,128)(2,1)S(1)}, u32[]{:S(2)}, u32[]{:S(2)}) %collective-permute-start) | collective-permute-done | bytes 524320 | tf_op jit(solution)/shard_map/ppermute | solution.py:200
  11.6 1.1 %broadcast_select_fusion.one_ref = bf16[512,512]{1,0:T(8,128)(2,1)S(1)} fusion(bf16[512,512]{1,0:T(8,128)(2,1)S(1)} %collective-permute-done, pred[]{:T(512)S(6)} %eq.3, bf16[1,1,512,512]{3,2,1,0:T(8,128)(2,1)} %param.2), kind=kLoop, calls=%fused_computation | loop fusion | flops 262144 | bytes 1572865 | tf_op jit(solution)/shard_map/jit(_where)/select_n | solution.py:201
  12.7 1.9 %collective-permute-start.1 = (bf16[512,512]{1,0:T(8,128)(2,1)S(1)}, bf16[512,512]{1,0:T(8,128)(2,1)S(1)}, u32[]{:S(2)}, u32[]{:S(2)}) collective-permute-start(bf16[512,512]{1,0:T(8,128)(2,1)S(1)} %broadcast_select_fusion.one_ref), channel_id=1, source_target_pairs={{0,1},{1,0},{2,3},{3,2},{4,5},{5,4},{6,7},{7,6},{8,9},{9,8},{10,11... | collective-permute-start | bytes 1572872 | tf_op jit(solution)/shard_map/ppermute | solution.py:202
  14.7 1.9 %collective-permute-done.1.two_ref = bf16[512,512]{1,0:T(8,128)(2,1)S(1)} collective-permute-done((bf16[512,512]{1,0:T(8,128)(2,1)S(1)}, bf16[512,512]{1,0:T(8,128)(2,1)S(1)}, u32[]{:S(2)}, u32[]{:S(2)}) %collective-permute-start.1) | collective-permute-done | bytes 524320 | tf_op jit(solution)/shard_map/ppermute | solution.py:202
  16.5 0.7 pack.1
  17.2 31.6 %all_to_all.15 = bf16[16,136,128]{2,1,0:T(8,128)(2,1)S(1)} all-to-all(bf16[16,136,128]{2,1,0:T(8,128)(2,1)S(1)} %pack.1), channel_id=1, replica_groups=mesh['q'=2,'p'=2,'z'=8,'x'=4,'h'=2,'c'=2] {'q','z'}, dimensions={0} | all-to-all | bytes 1114112 | tf_op jit(solution)/shard_map/all_to_all | solution.py:210
  48.8 0.1 reduce_sum.12
  48.9 0.1 broadcast_in_dim.4
  49.0 21.0 %all_to_all.16.stat_ref.mine_ref = bf16[16,136,128]{2,1,0:T(8,128)(2,1)S(1)} all-to-all(bf16[16,136,128]{2,1,0:T(8,128)(2,1)S(1)} %broadcast_in_dim.4), channel_id=1, replica_groups=mesh['q'=2,'p'=2,'z'=8,'x'=4,'h'=2,'c'=2] {'q','z'}, dimensions={0} | all-to-all | bytes 1114112 | tf_op jit(solution)/shard_map/all_to_all | solution.py:174
  70.0 3.2 %root.1.root_ref = bf16[512,512]{1,0:T(8,128)(2,1)S(1)} custom-call(bf16[16,136,128]{2,1,0:T(8,128)(2,1)S(1)} %all_to_all.16.stat_ref.mine_ref), custom_call_target="tpu_custom_call" | custom-call | tf_op jit(solution)/shard_map/root/pallas_call | solution.py:214
  73.2 4.7 %collective-permute-start.3 = (bf16[512,512]{1,0:T(8,128)(2,1)S(1)}, bf16[512,512]{1,0:T(8,128)(2,1)S(1)}, u32[]{:S(2)}, u32[]{:S(2)}) collective-permute-start(bf16[512,512]{1,0:T(8,128)(2,1)S(1)} %root.1.root_ref), channel_id=1, source_target_pairs={{0,1},{1,0},{2,3},{3,2},{4,5},{5,4},{6,7},{7,6},{8,9},{9,8},{10,11... | collective-permute-start | bytes 1572872 | tf_op jit(solution)/shard_map/ppermute | solution.py:221
  78.0 1.9 %collective-permute-start.2 = (bf16[16,64,128]{2,1,0:T(8,128)(2,1)S(1)}, bf16[16,64,128]{2,1,0:T(8,128)(2,1)S(1)}, u32[]{:S(2)}, u32[]{:S(2)}) collective-permute-start(bf16[16,64,128]{2,1,0:T(8,128)(2,1)S(1)} %slice.4), channel_id=1, source_target_pairs={{0,1},{1,0},{2,3},{3,2},{4,5},{5,4},{6,7},{7,6},{8,9},{9,8},{10,11... | collective-permute-start | bytes 786440 | tf_op jit(solution)/shard_map/ppermute | solution.py:213
  80.6 0.6 pad_add_fusion.1.scalar_ref
  81.2 0.2 collective-permute-done.2.half_ref
  81.4 0.0 collective-permute-done.3.other_ref
  81.4 2.5 %apply.1 = (f32[16,512]{1,0:T(8,128)S(1)}, f32[32,1,128]{2,1,0:T(1,128)}) custom-call(s32[3]{0:T(128)} %pad_add_fusion.1.scalar_ref, bf16[16,136,128]{2,1,0:T(8,128)(2,1)S(1)} %all_to_all.16.stat_ref.mine_ref, bf16[16,64,128]{2,1,0:T(8,128)(2,1)S(1)} %collective-permute-done.2.half_ref, bf16[512,512]{1,0:T(8,128)(2,1)S(1)} %root.1.root_ref, ...), custom_call_target="tpu_custom_call" | custom-call | tf_op jit(solution)/shard_map/apply/pallas_call | solution.py:225
  83.9 6.1 %all-to-all-start.2 = ((f32[32,1,128]{2,1,0:T(1,128)}), f32[32,1,128]{2,1,0:T(1,128)S(1)}, u32[]{:S(2)}, u32[]{:S(2)}) async-start(f32[32,1,128]{2,1,0:T(1,128)} %get-tuple-element.7), calls=%async_computation.2 | async-start | bytes 32768 | tf_op jit(solution)/shard_map/all_to_all | solution.py:237
  90.0 3.5 %collective-permute-start.4 = (f32[16,512]{1,0:T(8,128)S(1)}, f32[16,512]{1,0:T(8,128)S(1)}, u32[]{:S(2)}, u32[]{:S(2)}) collective-permute-start(f32[16,512]{1,0:T(8,128)S(1)} %get-tuple-element.8.rows_ref), channel_id=1, source_target_pairs={{1,128},{128,1},{3,130},{130,3},{5,132},{132,5},{7,134},{134,7},{9... | collective-permute-start | bytes 98312 | tf_op jit(solution)/shard_map/ppermute | solution.py:236
  93.6 0.6 pad_add_fusion.scalar_ref
  94.2 3.4 %all-to-all-done.2.notes_ref = f32[32,1,128]{2,1,0:T(1,128)S(1)} async-done(((f32[32,1,128]{2,1,0:T(1,128)}), f32[32,1,128]{2,1,0:T(1,128)S(1)}, u32[]{:S(2)}, u32[]{:S(2)}) %all-to-all-start.2) | async-done | bytes 16416 | tf_op jit(solution)/shard_map/all_to_all | solution.py:237
  97.5 0.0 collective-permute-done.4.moved_ref
  97.5 1.5 %scale.1 = bf16[16,512]{1,0:T(8,128)(2,1)} custom-call(s32[2]{0:T(128)} %pad_add_fusion.scalar_ref, f32[32,1,128]{2,1,0:T(1,128)S(1)} %all-to-all-done.2.notes_ref, f32[16,512]{1,0:T(8,128)S(1)} %get-tuple-element.8.rows_ref, f32[16,512]{1,0:T(8,128)S(1)} %collective-permute-done.4.moved_ref), custom_call_target="tpu_custom_call" | custom-call | tf_op jit(solution)/shard_map/scale/pallas_call | solution.py:238
  (1 shorter events, 0.0 us)
Async XLA Ops:
  0.0 11.6 %collective-permute-start = (bf16[512,512]{1,0:T(8,128)(2,1)}, bf16[512,512]{1,0:T(8,128)(2,1)S(1)}, u32[]{:S(2)}, u32[]{:S(2)}) collective-permute-start(bf16[512,512]{1,0:T(8,128)(2,1)} %bitcast.9), channel_id=1, source_target_pairs={{1,128},{128,1},{3,130},{130,3},{5,132},{132,5},{7,134},{134,7},{9... | collective-permute-start | bytes 1572872 | tf_op jit(solution)/shard_map/ppermute | solution.py:200
  12.7 3.8 %collective-permute-start.1 = (bf16[512,512]{1,0:T(8,128)(2,1)S(1)}, bf16[512,512]{1,0:T(8,128)(2,1)S(1)}, u32[]{:S(2)}, u32[]{:S(2)}) collective-permute-start(bf16[512,512]{1,0:T(8,128)(2,1)S(1)} %broadcast_select_fusion.one_ref), channel_id=1, source_target_pairs={{0,1},{1,0},{2,3},{3,2},{4,5},{5,4},{6,7},{7,6},{8,9},{9,8},{10,11... | collective-permute-start | bytes 1572872 | tf_op jit(solution)/shard_map/ppermute | solution.py:202
  73.2 8.2 %collective-permute-start.3 = (bf16[512,512]{1,0:T(8,128)(2,1)S(1)}, bf16[512,512]{1,0:T(8,128)(2,1)S(1)}, u32[]{:S(2)}, u32[]{:S(2)}) collective-permute-start(bf16[512,512]{1,0:T(8,128)(2,1)S(1)} %root.1.root_ref), channel_id=1, source_target_pairs={{0,1},{1,0},{2,3},{3,2},{4,5},{5,4},{6,7},{7,6},{8,9},{9,8},{10,11... | collective-permute-start | bytes 1572872 | tf_op jit(solution)/shard_map/ppermute | solution.py:221
  78.0 3.4 %collective-permute-start.2 = (bf16[16,64,128]{2,1,0:T(8,128)(2,1)S(1)}, bf16[16,64,128]{2,1,0:T(8,128)(2,1)S(1)}, u32[]{:S(2)}, u32[]{:S(2)}) collective-permute-start(bf16[16,64,128]{2,1,0:T(8,128)(2,1)S(1)} %slice.4), channel_id=1, source_target_pairs={{0,1},{1,0},{2,3},{3,2},{4,5},{5,4},{6,7},{7,6},{8,9},{9,8},{10,11... | collective-permute-start | bytes 786440 | tf_op jit(solution)/shard_map/ppermute | solution.py:213
  83.9 13.6 %all-to-all-start.2 = ((f32[32,1,128]{2,1,0:T(1,128)}), f32[32,1,128]{2,1,0:T(1,128)S(1)}, u32[]{:S(2)}, u32[]{:S(2)}) async-start(f32[32,1,128]{2,1,0:T(1,128)} %get-tuple-element.7), calls=%async_computation.2 | async-start | bytes 32768 | tf_op jit(solution)/shard_map/all_to_all | solution.py:237
  90.0 7.5 %collective-permute-start.4 = (f32[16,512]{1,0:T(8,128)S(1)}, f32[16,512]{1,0:T(8,128)S(1)}, u32[]{:S(2)}, u32[]{:S(2)}) collective-permute-start(f32[16,512]{1,0:T(8,128)S(1)} %get-tuple-element.8.rows_ref), channel_id=1, source_target_pairs={{1,128},{128,1},{3,130},{130,3},{5,132},{132,5},{7,134},{134,7},{9... | collective-permute-start | bytes 98312 | tf_op jit(solution)/shard_map/ppermute | solution.py:236

commit v3 on v2

--- a/solution.py
+++ b/solution.py
@@ -34,8 +34,14 @@
     return row, col
 
 
-def pack_kernel(role_ref, one_ref, two_ref, out_ref):
+def fetch_kernel(layer_ref, grad_ref, copy_ref, label_ref):
+    copy_ref[...] = grad_ref[...]
+    label_ref[...] = jnp.full(label_ref.shape, layer_ref[0].astype(jnp.float32), jnp.float32)
+
+
+def pack_kernel(one_ref, two_ref, out_ref):
     row, col = triangle()
+    own_role = lax.axis_index("c")
 
     def pack(role):
         upper = cross = lower = 0.0
@@ -64,7 +70,7 @@
             out_ref[:, start : start + SLAB, :] = total[:, c * LANE : (c + 1) * LANE].reshape(N_PEER, SLAB, LANE)
 
     for role in range(2):
-        pl.when(role_ref[0] == role)(lambda role=role: pack(role))
+        pl.when(own_role == role)(lambda role=role: pack(role))
 
 
 def inverse_root(statistic_parts, row, col):
@@ -114,51 +120,41 @@
     upper = jnp.where(row <= col, folded, flipped)
     lower = jnp.where(row > col, folded, flipped)
     lower = jnp.where(row == col, diagonal, lower)
-    out_ref[...] = inverse_root((upper, cross, lower), row, col)
-
-
-def apply_kernel(scalar_ref, mine_ref, half_ref, root_ref, other_ref, rows_ref, note_ref, whole_ref):
-    role = scalar_ref[0]
-    start = BODY + DIAG
-
-    def wide(ref, offset):
-        return jnp.concatenate(
-            [
-                ref[:, offset + c * SLAB : offset + (c + 1) * SLAB, :].reshape(H, LANE)
-                for c in range(COLS)
-            ],
-            axis=1,
-        )
-
-    def apply(left_ref, right_ref, top, bottom):
-        right = right_ref[...]
-        middle = dot(left_ref[:, :H], top) + dot(left_ref[:, H:], bottom)
+    for c in range(COLS):
+        start = BODY + DIAG + c * SLAB
+        out_ref[B:, c * LANE : (c + 1) * LANE] = stat_ref[:, start : start + SLAB, :].reshape(H, LANE)
+    out_ref[:B] = inverse_root((upper, cross, lower), row, col)
+
+
+def apply_kernel(label_ref, mine_ref, other_ref, rows_ref, note_ref, whole_ref):
+    role = lax.axis_index("c")
+    keeper = role == lax.axis_index("p")
+
+    def apply(left_ref, right_ref):
+        middle = dot(left_ref[:B, :H], left_ref[B:]) + dot(left_ref[:B, H:], right_ref[B:])
+        right = right_ref[:B]
         high = middle.astype(jnp.bfloat16)
         low = (middle - high.astype(jnp.float32)).astype(jnp.bfloat16)
         whole = (dot(high, right) + dot(low, right)) * (1.0 / N_DP)
         whole_ref[...] = whole
         energy = jnp.sum(whole * whole)
         lane = lax.broadcasted_iota(jnp.int32, note_ref.shape, 2)
-        layer = scalar_ref[2].astype(jnp.float32)
+        layer = jnp.where(keeper, label_ref[0:1, :], -1.0)[None]
         note_ref[...] = jnp.where(lane == 0, energy, layer)
 
-    @pl.when(role == 0)
-    def _():
-        apply(root_ref, other_ref, wide(mine_ref, start), wide(half_ref, 0))
-
-    @pl.when(role == 1)
-    def _():
-        apply(other_ref, root_ref, wide(half_ref, 0), wide(mine_ref, start))
-
-    rows_ref[...] = whole_ref[pl.ds(scalar_ref[1] * ROWS, ROWS), :]
-
-
-def scale_kernel(scalar_ref, notes_ref, rows_ref, moved_ref, out_ref):
+    pl.when(role == 0)(lambda: apply(mine_ref, other_ref))
+    pl.when(role == 1)(lambda: apply(other_ref, mine_ref))
+    place = (lax.axis_index("q") * 2 + role) * 8 + lax.axis_index("z")
+    rows_ref[...] = whole_ref[pl.ds(place * ROWS, ROWS), :]
+
+
+def scale_kernel(label_ref, notes_ref, rows_ref, moved_ref, out_ref):
+    keeper = lax.axis_index("c") == lax.axis_index("p")
     notes = notes_ref[...]
-    mine = notes[:, 0, 1:2] == scalar_ref[0].astype(jnp.float32)
+    mine = notes[:, 0, 1:2] == label_ref[0:1, 0:1]
     energy = jnp.sum(jnp.where(mine, notes[:, 0, 0:1], 0.0), axis=0, keepdims=True)
     count = jnp.sum(jnp.where(mine, float(B * B), 0.0), axis=0, keepdims=True)
-    rows = jnp.where(scalar_ref[1] == 1, rows_ref[...], moved_ref[...])
+    rows = jnp.where(keeper, rows_ref[...], moved_ref[...])
     out_ref[...] = (rows * lax.rsqrt(energy / count + 1e-06)).astype(jnp.bfloat16)
 
 
@@ -195,53 +191,55 @@
 
 def per_device(gradients, block_layer):
     own = gradients[0, 0]
-    role = lax.axis_index("c")
-    keeper = role == lax.axis_index("p")
+    keeper = lax.axis_index("c") == lax.axis_index("p")
     swapped = lax.ppermute(own, CHIP_PAIR, SWAP)
-    one = jnp.where(keeper, own, swapped)
+    local, label = pl.pallas_call(
+        fetch_kernel,
+        out_shape=(pltpu.VMEM((B, B), jnp.bfloat16), pltpu.VMEM((8, LANE), jnp.float32)),
+        in_specs=[SMEM, VMEM],
+        out_specs=(VMEM, VMEM),
+        name="fetch",
+    )(block_layer, own)
+    one = jnp.where(keeper, local, swapped)
     two = lax.ppermute(one, "c", ACROSS)
     packed = pl.pallas_call(
         pack_kernel,
         out_shape=pltpu.VMEM((N_PEER, 2 * BODY + DIAG, LANE), jnp.bfloat16),
-        in_specs=[SMEM, VMEM, VMEM],
+        in_specs=[VMEM, VMEM],
         out_specs=VMEM,
         name="pack",
-    )(role[None], near(one), near(two))
+    )(near(one), near(two))
     arrived = lax.all_to_all(packed, PEERS, 0, 0, tiled=True)
     mine = jnp.sum(arrived.astype(jnp.float32), axis=0).astype(jnp.bfloat16)
     everything = to_all(mine, PEERS, N_PEER)
-    half = lax.ppermute(everything[:, BODY + DIAG :], "c", ACROSS)
-    root = pl.pallas_call(
+    solved = pl.pallas_call(
         root_kernel,
-        out_shape=pltpu.VMEM((B, B), jnp.bfloat16),
+        out_shape=pltpu.VMEM((B + H, B), jnp.bfloat16),
         in_specs=[VMEM],
         out_specs=VMEM,
         name="root",
     )(near(everything))
-    other = lax.ppermute(root, "c", ACROSS)
-    place = (lax.axis_index("q") * 2 + role) * 8 + lax.axis_index("z")
-    layer = jnp.where(keeper, block_layer[0], -1)
-    scalars = jnp.stack([role, place, layer]).astype(jnp.int32)
+    other = lax.ppermute(solved, "c", ACROSS)
     rows, note = pl.pallas_call(
         apply_kernel,
         out_shape=(
             pltpu.VMEM((ROWS, B), jnp.float32),
             pltpu.VMEM((N_NOTE, 1, LANE), jnp.float32),
         ),
-        in_specs=[SMEM, VMEM, VMEM, VMEM, VMEM],
+        in_specs=[VMEM, VMEM, VMEM],
         out_specs=(VMEM, VMEM),
         scratch_shapes=[pltpu.VMEM((B, B), jnp.float32)],
         name="apply",
-    )(scalars, near(everything), near(half), near(root), near(other))
+    )(near(label), near(solved), near(other))
+    notes = lax.all_to_all(note, NOTE_AXES, 0, 0, tiled=True, axis_index_groups=note_groups())
     moved = lax.ppermute(rows, CHIP_PAIR, SWAP)
-    notes = lax.all_to_all(note, NOTE_AXES, 0, 0, tiled=True, axis_index_groups=note_groups())
     update = pl.pallas_call(
         scale_kernel,
         out_shape=jax.ShapeDtypeStruct((ROWS, B), jnp.bfloat16),
-        in_specs=[SMEM, VMEM, VMEM, VMEM],
+        in_specs=[VMEM, VMEM, VMEM, VMEM],
         out_specs=VMEM,
         name="scale",
-    )(jnp.stack([block_layer[0], keeper.astype(jnp.int32)]), near(notes), near(rows), near(moved))
+    )(near(label), near(notes), near(rows), near(moved))
     return update[None]
 
 

time: 100 us -> 98.6 us (0.986)
  blocking collectives: 52.6 us -> 66.9 us
  starting transfers between devices: 22.8 us -> 13.5 us
  waiting for transfers between devices: 12.5 us -> 9.09 us
  other arithmetic: 2.4 us -> 0.15 us
    all_to_all x0 -> x1, blocking collectives: none -> 14.3 us  [per_device(): lax.all_to_all(note, NOTE_AXES, 0, 0, tiled=True, axis_index_groups=note_...]
    all_to_all x1 -> x0, starting transfers between devices: 6.09 us -> none  [per_device(): lax.all_to_all(note, NOTE_AXES, 0, 0, tiled=True, axis_index_groups=note_...]
    all_to_all x1 -> x0, waiting for transfers between devices: 3.36 us -> none  [per_device(): lax.all_to_all(note, NOTE_AXES, 0, 0, tiled=True, axis_index_groups=note_...]
    ppermute x2 -> x1, starting transfers between devices: 6.64 us -> 4.67 us  [per_device(): other = lax.ppermute(solved, 'c', ACROSS)]
    ppermute x1, waiting for transfers between devices: 7.05 us -> 5.32 us  [per_device(): swapped = lax.ppermute(own, CHIP_PAIR, SWAP)]
    ppermute x2 -> x1, waiting for transfers between devices: 0.2 us -> 1.89 us  [per_device(): other = lax.ppermute(solved, 'c', ACROSS)]
    pallas_call x1, Pallas kernels: 2.52 us -> 1.26 us  [per_device(): pl.pallas_call(apply_kernel, out_shape=(pltpu.VMEM((ROWS, B), jnp.float32...]
    ppermute x1, starting transfers between devices: 3.55 us -> 2.3 us  [per_device(): moved = lax.ppermute(rows, CHIP_PAIR, SWAP)]
  transfers between devices with their start and end apart: 6 -> 4, of which waited for: 4 -> 3; matrix products, arithmetic and copies ran while one was open for 1% -> 0% of each run, Pallas kernels for 0% -> 1%
where the time goes in v3:
time: 98.6 us; the launch traced here: 97.5 us
  blocking collectives  66.9 us (68%)
  starting transfers between devices  13.5 us (14%)
  waiting for transfers between devices  9.09 us (9%)
  Pallas kernels  7.02 us (7%)
    all_to_all x1, blocking collectives, per_device(): arrived = lax.all_to_all(packed, PEERS, 0, 0, tiled=True)  31.6 us
    all_to_all x1, blocking collectives, to_all(): lax.all_to_all(jnp.broadcast_to(x[None], (size, *x.shape)), axes, 0, 0, t...  21.1 us
    all_to_all x1, blocking collectives, per_device(): lax.all_to_all(note, NOTE_AXES, 0, 0, tiled=True, axis_index_groups=note_...  14.3 us
    ppermute x1, waiting for transfers between devices, per_device(): swapped = lax.ppermute(own, CHIP_PAIR, SWAP)  5.32 us
    ppermute x1, starting transfers between devices, per_device(): other = lax.ppermute(solved, 'c', ACROSS)  4.67 us
    ppermute x1, starting transfers between devices, per_device(): swapped = lax.ppermute(own, CHIP_PAIR, SWAP)  4.57 us
    pallas_call x1, Pallas kernels, per_device(): pl.pallas_call(root_kernel, out_shape=pltpu.VMEM((B + H, B), jnp.bfloat16...  3.23 us
    ppermute x1, starting transfers between devices, per_device(): moved = lax.ppermute(rows, CHIP_PAIR, SWAP)  2.3 us
  transfers between devices with their start and end apart: 4, of which 3 were waited for; matrix products, arithmetic and copies ran while one was open for 0% of the time, Pallas kernels for 1%

profile of v3, /device:TPU:1, one launch (start us, length us, event | category | flops | bytes accessed | tf_op | source)
XLA Modules:
  0.0 97.5 jit_solution(11582332101417026110)
XLA Ops:
  0.0 4.6 %collective-permute-start = (bf16[512,512]{1,0:T(8,128)(2,1)}, bf16[512,512]{1,0:T(8,128)(2,1)S(1)}, u32[]{:S(2)}, u32[]{:S(2)}) collective-permute-start(bf16[512,512]{1,0:T(8,128)(2,1)} %bitcast.2), channel_id=1, source_target_pairs={{1,128},{128,1},{3,130},{130,3},{5,132},{132,5},{7,134},{134,7},{9... | collective-permute-start | bytes 1572872 | tf_op jit(solution)/shard_map/ppermute | solution.py:195
  5.2 1.1 %fetch.1 = (bf16[512,512]{1,0:T(8,128)(2,1)S(1)}, f32[8,128]{1,0:T(8,128)S(1)}) custom-call(s32[1]{0:T(128)S(6)} %copy.3.layer_ref, bf16[512,512]{1,0:T(8,128)(2,1)} %bitcast.3), custom_call_target="tpu_custom_call" | custom-call | tf_op jit(solution)/shard_map/fetch/pallas_call | solution.py:196
  6.3 5.3 %collective-permute-done = bf16[512,512]{1,0:T(8,128)(2,1)S(1)} collective-permute-done((bf16[512,512]{1,0:T(8,128)(2,1)}, bf16[512,512]{1,0:T(8,128)(2,1)S(1)}, u32[]{:S(2)}, u32[]{:S(2)}) %collective-permute-start) | collective-permute-done | bytes 524320 | tf_op jit(solution)/shard_map/ppermute | solution.py:195
  11.6 0.1 broadcast_select_fusion.one_ref
  11.7 1.9 %collective-permute-start.1 = (bf16[512,512]{1,0:T(8,128)(2,1)S(1)}, bf16[512,512]{1,0:T(8,128)(2,1)S(1)}, u32[]{:S(2)}, u32[]{:S(2)}) collective-permute-start(bf16[512,512]{1,0:T(8,128)(2,1)S(1)} %broadcast_select_fusion.one_ref), channel_id=1, source_target_pairs={{0,1},{1,0},{2,3},{3,2},{4,5},{5,4},{6,7},{7,6},{8,9},{9,8},{10,11... | collective-permute-start | bytes 1572872 | tf_op jit(solution)/shard_map/ppermute | solution.py:204
  13.6 1.9 %collective-permute-done.1.two_ref = bf16[512,512]{1,0:T(8,128)(2,1)S(1)} collective-permute-done((bf16[512,512]{1,0:T(8,128)(2,1)S(1)}, bf16[512,512]{1,0:T(8,128)(2,1)S(1)}, u32[]{:S(2)}, u32[]{:S(2)}) %collective-permute-start.1) | collective-permute-done | bytes 524320 | tf_op jit(solution)/shard_map/ppermute | solution.py:204
  15.5 0.7 pack.1
  16.2 31.6 %all_to_all.15 = bf16[16,136,128]{2,1,0:T(8,128)(2,1)S(1)} all-to-all(bf16[16,136,128]{2,1,0:T(8,128)(2,1)S(1)} %pack.1), channel_id=1, replica_groups=mesh['q'=2,'p'=2,'z'=8,'x'=4,'h'=2,'c'=2] {'q','z'}, dimensions={0} | all-to-all | bytes 1114112 | tf_op jit(solution)/shard_map/all_to_all | solution.py:212
  47.8 0.1 reduce_sum.12
  47.9 0.1 broadcast_in_dim.4
  48.0 21.1 %all_to_all.16.stat_ref = bf16[16,136,128]{2,1,0:T(8,128)(2,1)S(1)} all-to-all(bf16[16,136,128]{2,1,0:T(8,128)(2,1)S(1)} %broadcast_in_dim.4), channel_id=1, replica_groups=mesh['q'=2,'p'=2,'z'=8,'x'=4,'h'=2,'c'=2] {'q','z'}, dimensions={0} | all-to-all | bytes 1114112 | tf_op jit(solution)/shard_map/all_to_all | solution.py:170
  69.0 3.2 %root.1.mine_ref = bf16[768,512]{1,0:T(8,128)(2,1)S(1)} custom-call(bf16[16,136,128]{2,1,0:T(8,128)(2,1)S(1)} %all_to_all.16.stat_ref), custom_call_target="tpu_custom_call" | custom-call | tf_op jit(solution)/shard_map/root/pallas_call | solution.py:215
  72.3 4.7 %collective-permute-start.2 = (bf16[768,512]{1,0:T(8,128)(2,1)S(1)}, bf16[768,512]{1,0:T(8,128)(2,1)S(1)}, u32[]{:S(2)}, u32[]{:S(2)}) collective-permute-start(bf16[768,512]{1,0:T(8,128)(2,1)S(1)} %root.1.mine_ref), channel_id=1, source_target_pairs={{0,1},{1,0},{2,3},{3,2},{4,5},{5,4},{6,7},{7,6},{8,9},{9,8},{10,11... | collective-permute-start | bytes 2359304 | tf_op jit(solution)/shard_map/ppermute | solution.py:222
  77.0 1.9 %collective-permute-done.2.other_ref = bf16[768,512]{1,0:T(8,128)(2,1)S(1)} collective-permute-done((bf16[768,512]{1,0:T(8,128)(2,1)S(1)}, bf16[768,512]{1,0:T(8,128)(2,1)S(1)}, u32[]{:S(2)}, u32[]{:S(2)}) %collective-permute-start.2) | collective-permute-done | bytes 786464 | tf_op jit(solution)/shard_map/ppermute | solution.py:222
  78.8 1.3 %apply.1 = (f32[16,512]{1,0:T(8,128)S(1)}, f32[32,1,128]{2,1,0:T(1,128)S(1)}) custom-call(f32[8,128]{1,0:T(8,128)S(1)} %get-tuple-element.9.label_ref, bf16[768,512]{1,0:T(8,128)(2,1)S(1)} %root.1.mine_ref, bf16[768,512]{1,0:T(8,128)(2,1)S(1)} %collective-permute-done.2.other_ref), custom_call_target="tpu_custom_call" | custom-call | tf_op jit(solution)/shard_map/apply/pallas_call | solution.py:223
  80.1 2.3 %collective-permute-start.3 = (f32[16,512]{1,0:T(8,128)S(1)}, f32[16,512]{1,0:T(8,128)S(1)}, u32[]{:S(2)}, u32[]{:S(2)}) collective-permute-start(f32[16,512]{1,0:T(8,128)S(1)} %get-tuple-element.12.rows_ref), channel_id=1, source_target_pairs={{1,128},{128,1},{3,130},{130,3},{5,132},{132,5},{7,134},{134,7},{9... | collective-permute-start | bytes 98312 | tf_op jit(solution)/shard_map/ppermute | solution.py:235
  82.4 14.3 %all_to_all.17.notes_ref = f32[32,1,128]{2,1,0:T(1,128)S(1)} all-to-all(f32[32,1,128]{2,1,0:T(1,128)S(1)} %get-tuple-element.11), channel_id=1, replica_groups={{0,1,258,259,4,5,262,263,8,9,266,267,12,13,270,271,128,129,386,387,132,..., dimensions={0} | all-to-all | bytes 32768 | tf_op jit(solution)/shard_map/all_to_all | solution.py:234
  96.7 0.0 collective-permute-done.3.moved_ref
  96.7 0.8 scale.1
Async XLA Ops:
  0.0 11.6 %collective-permute-start = (bf16[512,512]{1,0:T(8,128)(2,1)}, bf16[512,512]{1,0:T(8,128)(2,1)S(1)}, u32[]{:S(2)}, u32[]{:S(2)}) collective-permute-start(bf16[512,512]{1,0:T(8,128)(2,1)} %bitcast.2), channel_id=1, source_target_pairs={{1,128},{128,1},{3,130},{130,3},{5,132},{132,5},{7,134},{134,7},{9... | collective-permute-start | bytes 1572872 | tf_op jit(solution)/shard_map/ppermute | solution.py:195
  11.7 3.8 %collective-permute-start.1 = (bf16[512,512]{1,0:T(8,128)(2,1)S(1)}, bf16[512,512]{1,0:T(8,128)(2,1)S(1)}, u32[]{:S(2)}, u32[]{:S(2)}) collective-permute-start(bf16[512,512]{1,0:T(8,128)(2,1)S(1)} %broadcast_select_fusion.one_ref), channel_id=1, source_target_pairs={{0,1},{1,0},{2,3},{3,2},{4,5},{5,4},{6,7},{7,6},{8,9},{9,8},{10,11... | collective-permute-start | bytes 1572872 | tf_op jit(solution)/shard_map/ppermute | solution.py:204
  72.3 6.6 %collective-permute-start.2 = (bf16[768,512]{1,0:T(8,128)(2,1)S(1)}, bf16[768,512]{1,0:T(8,128)(2,1)S(1)}, u32[]{:S(2)}, u32[]{:S(2)}) collective-permute-start(bf16[768,512]{1,0:T(8,128)(2,1)S(1)} %root.1.mine_ref), channel_id=1, source_target_pairs={{0,1},{1,0},{2,3},{3,2},{4,5},{5,4},{6,7},{7,6},{8,9},{9,8},{10,11... | collective-permute-start | bytes 2359304 | tf_op jit(solution)/shard_map/ppermute | solution.py:222
  80.1 16.6 %collective-permute-start.3 = (f32[16,512]{1,0:T(8,128)S(1)}, f32[16,512]{1,0:T(8,128)S(1)}, u32[]{:S(2)}, u32[]{:S(2)}) collective-permute-start(f32[16,512]{1,0:T(8,128)S(1)} %get-tuple-element.12.rows_ref), channel_id=1, source_target_pairs={{1,128},{128,1},{3,130},{130,3},{5,132},{132,5},{7,134},{134,7},{9... | collective-permute-start | bytes 98312 | tf_op jit(solution)/shard_map/ppermute | solution.py:235

commit v4 on v3

--- a/solution.py
+++ b/solution.py
@@ -10,13 +10,13 @@
 OWNER = ("x", "h", "c")
 PEERS = ("q", "z")
 CHIP_PAIR = ("p", "c")
-NOTE_AXES = ("q", "p", "x", "h", "c")
+NOTE_AXES = ("q", "p", "x", "h")
 B = 512
 H = B // 2
 LANE = 128
 N_DP = 32
 N_PEER = 16
-N_NOTE = 32
+N_NOTE = 16
 ROWS = B // N_DP
 SLAB = H // N_PEER
 COLS = B // LANE
@@ -106,7 +106,7 @@
     return (jnp.where(full_row == full_col, rest + 1.953125, rest) * root_scale).astype(jnp.bfloat16)
 
 
-def root_kernel(stat_ref, out_ref):
+def root_kernel(label_ref, stat_ref, out_ref):
     row, col = triangle()
     parts = [
         stat_ref[:, c * SLAB : (c + 1) * SLAB, :].reshape(H, LANE).astype(jnp.float32)
@@ -122,30 +122,45 @@
     lower = jnp.where(row == col, diagonal, lower)
     for c in range(COLS):
         start = BODY + DIAG + c * SLAB
-        out_ref[B:, c * LANE : (c + 1) * LANE] = stat_ref[:, start : start + SLAB, :].reshape(H, LANE)
+        out_ref[B : B + H, c * LANE : (c + 1) * LANE] = stat_ref[:, start : start + SLAB, :].reshape(H, LANE)
+    out_ref[B + H :, :LANE] = label_ref[...].astype(jnp.bfloat16)
+    out_ref[B + H :, LANE:] = jnp.zeros((DIAG, B - LANE), jnp.bfloat16)
     out_ref[:B] = inverse_root((upper, cross, lower), row, col)
 
 
-def apply_kernel(label_ref, mine_ref, other_ref, rows_ref, note_ref, whole_ref):
+def by_role(mine_ref, other_ref, apply):
     role = lax.axis_index("c")
-    keeper = role == lax.axis_index("p")
+    pl.when(role == 0)(lambda: apply(mine_ref, other_ref))
+    pl.when(role == 1)(lambda: apply(other_ref, mine_ref))
+
+
+def energy_kernel(label_ref, mine_ref, other_ref, note_ref):
+    keeper = lax.axis_index("c") == lax.axis_index("p")
 
     def apply(left_ref, right_ref):
-        middle = dot(left_ref[:B, :H], left_ref[B:]) + dot(left_ref[:B, H:], right_ref[B:])
-        right = right_ref[:B]
+        middle = dot(left_ref[:B, :H], left_ref[B : B + H]) + dot(left_ref[:B, H:], right_ref[B : B + H])
+        whole = dot(middle.astype(jnp.bfloat16), right_ref[:B]) * (1.0 / N_DP)
+        energy = jnp.sum(whole * whole)
+        lane = lax.broadcasted_iota(jnp.int32, note_ref.shape, 2)
+        passed = other_ref[B + H : B + H + DIAG, :LANE].astype(jnp.float32)
+        layer = jnp.where(keeper, label_ref[0:1, :], passed[0:1])[None]
+        note_ref[...] = jnp.where(lane == 0, energy, layer)
+
+    by_role(mine_ref, other_ref, apply)
+
+
+def rows_kernel(mine_ref, other_ref, rows_ref):
+    place = (lax.axis_index("q") * 2 + lax.axis_index("c")) * 8 + lax.axis_index("z")
+
+    def apply(left_ref, right_ref):
+        left = left_ref[pl.ds(place * ROWS, ROWS), :]
+        middle = dot(left[:, :H], left_ref[B : B + H]) + dot(left[:, H:], right_ref[B : B + H])
         high = middle.astype(jnp.bfloat16)
         low = (middle - high.astype(jnp.float32)).astype(jnp.bfloat16)
-        whole = (dot(high, right) + dot(low, right)) * (1.0 / N_DP)
-        whole_ref[...] = whole
-        energy = jnp.sum(whole * whole)
-        lane = lax.broadcasted_iota(jnp.int32, note_ref.shape, 2)
-        layer = jnp.where(keeper, label_ref[0:1, :], -1.0)[None]
-        note_ref[...] = jnp.where(lane == 0, energy, layer)
-
-    pl.when(role == 0)(lambda: apply(mine_ref, other_ref))
-    pl.when(role == 1)(lambda: apply(other_ref, mine_ref))
-    place = (lax.axis_index("q") * 2 + role) * 8 + lax.axis_index("z")
-    rows_ref[...] = whole_ref[pl.ds(place * ROWS, ROWS), :]
+        both = dot(jnp.concatenate([high, low], axis=0), right_ref[:B])
+        rows_ref[...] = (both[:ROWS] + both[ROWS:]) * (1.0 / N_DP)
+
+    by_role(mine_ref, other_ref, apply)
 
 
 def scale_kernel(label_ref, notes_ref, rows_ref, moved_ref, out_ref):
@@ -171,18 +186,10 @@
 
 
 def note_groups():
-    groups = []
-    for q in range(2):
-        groups.append(
-            [
-                (((q ^ h) * 2 + p) * 4 + x) * 4 + h * 2 + c
-                for p in range(2)
-                for x in range(4)
-                for h in range(2)
-                for c in range(2)
-            ]
-        )
-    return groups
+    return [
+        [(((q ^ h) * 2 + p) * 4 + x) * 2 + h for p in range(2) for x in range(4) for h in range(2)]
+        for q in range(2)
+    ]
 
 
 SWAP = [(1, 2), (2, 1)]
@@ -214,24 +221,27 @@
     everything = to_all(mine, PEERS, N_PEER)
     solved = pl.pallas_call(
         root_kernel,
-        out_shape=pltpu.VMEM((B + H, B), jnp.bfloat16),
-        in_specs=[VMEM],
+        out_shape=pltpu.VMEM((B + H + DIAG, B), jnp.bfloat16),
+        in_specs=[VMEM, VMEM],
         out_specs=VMEM,
         name="root",
-    )(near(everything))
+    )(near(label), near(everything))
     other = lax.ppermute(solved, "c", ACROSS)
-    rows, note = pl.pallas_call(
-        apply_kernel,
-        out_shape=(
-            pltpu.VMEM((ROWS, B), jnp.float32),
-            pltpu.VMEM((N_NOTE, 1, LANE), jnp.float32),
-        ),
+    note = pl.pallas_call(
+        energy_kernel,
+        out_shape=pltpu.VMEM((N_NOTE, 1, LANE), jnp.float32),
         in_specs=[VMEM, VMEM, VMEM],
-        out_specs=(VMEM, VMEM),
-        scratch_shapes=[pltpu.VMEM((B, B), jnp.float32)],
-        name="apply",
+        out_specs=VMEM,
+        name="energy",
     )(near(label), near(solved), near(other))
     notes = lax.all_to_all(note, NOTE_AXES, 0, 0, tiled=True, axis_index_groups=note_groups())
+    rows = pl.pallas_call(
+        rows_kernel,
+        out_shape=pltpu.VMEM((ROWS, B), jnp.float32),
+        in_specs=[VMEM, VMEM],
+        out_specs=VMEM,
+        name="rows",
+    )(near(solved), near(other))
     moved = lax.ppermute(rows, CHIP_PAIR, SWAP)
     update = pl.pallas_call(
         scale_kernel,

time: 98.6 us -> 98.6 us (level)
    pallas_call x2 -> x3, Pallas kernels: 4.49 us -> 4.57 us  [the longest x1 3.24 us: per_device(): pl.pallas_call(root_kernel, out_shape=pltpu.VMEM((B + H + DIAG, B), jnp.b...]
  transfers between devices with their start and end apart: 4 -> 4, of which waited for: 3 -> 3; matrix products, arithmetic and copies ran while one was open for 0% -> 0% of each run, Pallas kernels for 1% -> 2%
where the time goes in v4:
time: 98.6 us; the launch traced here: 96.6 us
  blocking collectives  66 us (67%)
  starting transfers between devices  13.5 us (14%)
  waiting for transfers between devices  9.1 us (9%)
  Pallas kernels  7.1 us (7%)
    all_to_all x1, blocking collectives, per_device(): arrived = lax.all_to_all(packed, PEERS, 0, 0, tiled=True)  31.6 us
    all_to_all x1, blocking collectives, to_all(): lax.all_to_all(jnp.broadcast_to(x[None], (size, *x.shape)), axes, 0, 0, t...  21.1 us
    all_to_all x1, blocking collectives, per_device(): lax.all_to_all(note, NOTE_AXES, 0, 0, tiled=True, axis_index_groups=note_...  13.3 us
    ppermute x1, waiting for transfers between devices, per_device(): swapped = lax.ppermute(own, CHIP_PAIR, SWAP)  5.32 us
    ppermute x1, starting transfers between devices, per_device(): other = lax.ppermute(solved, 'c', ACROSS)  4.68 us
    ppermute x1, starting transfers between devices, per_device(): swapped = lax.ppermute(own, CHIP_PAIR, SWAP)  4.57 us
    pallas_call x1, Pallas kernels, per_device(): pl.pallas_call(root_kernel, out_shape=pltpu.VMEM((B + H + DIAG, B), jnp.b...  3.24 us
    ppermute x1, starting transfers between devices, per_device(): moved = lax.ppermute(rows, CHIP_PAIR, SWAP)  2.28 us
  transfers between devices with their start and end apart: 4, of which 3 were waited for; matrix products, arithmetic and copies ran while one was open for 0% of the time, Pallas kernels for 2%

profile of v4, /device:TPU:1, one launch (start us, length us, event | category | flops | bytes accessed | tf_op | source)
XLA Modules:
  0.0 96.6 jit_solution(17557753144238960060)
XLA Ops:
  0.0 4.6 %collective-permute-start = (bf16[512,512]{1,0:T(8,128)(2,1)}, bf16[512,512]{1,0:T(8,128)(2,1)S(1)}, u32[]{:S(2)}, u32[]{:S(2)}) collective-permute-start(bf16[512,512]{1,0:T(8,128)(2,1)} %bitcast.2), channel_id=1, source_target_pairs={{1,128},{128,1},{3,130},{130,3},{5,132},{132,5},{7,134},{134,7},{9... | collective-permute-start | bytes 1572872 | tf_op jit(solution)/shard_map/ppermute | solution.py:202
  5.2 1.1 %fetch.1 = (bf16[512,512]{1,0:T(8,128)(2,1)S(1)}, f32[8,128]{1,0:T(8,128)S(1)}) custom-call(s32[1]{0:T(128)S(6)} %copy.3.layer_ref, bf16[512,512]{1,0:T(8,128)(2,1)} %bitcast.3), custom_call_target="tpu_custom_call" | custom-call | tf_op jit(solution)/shard_map/fetch/pallas_call | solution.py:203
  6.3 5.3 %collective-permute-done = bf16[512,512]{1,0:T(8,128)(2,1)S(1)} collective-permute-done((bf16[512,512]{1,0:T(8,128)(2,1)}, bf16[512,512]{1,0:T(8,128)(2,1)S(1)}, u32[]{:S(2)}, u32[]{:S(2)}) %collective-permute-start) | collective-permute-done | bytes 524320 | tf_op jit(solution)/shard_map/ppermute | solution.py:202
  11.6 0.1 broadcast_select_fusion.one_ref
  11.7 1.9 %collective-permute-start.1 = (bf16[512,512]{1,0:T(8,128)(2,1)S(1)}, bf16[512,512]{1,0:T(8,128)(2,1)S(1)}, u32[]{:S(2)}, u32[]{:S(2)}) collective-permute-start(bf16[512,512]{1,0:T(8,128)(2,1)S(1)} %broadcast_select_fusion.one_ref), channel_id=1, source_target_pairs={{0,1},{1,0},{2,3},{3,2},{4,5},{5,4},{6,7},{7,6},{8,9},{9,8},{10,11... | collective-permute-start | bytes 1572872 | tf_op jit(solution)/shard_map/ppermute | solution.py:211
  13.6 1.9 %collective-permute-done.1.two_ref = bf16[512,512]{1,0:T(8,128)(2,1)S(1)} collective-permute-done((bf16[512,512]{1,0:T(8,128)(2,1)S(1)}, bf16[512,512]{1,0:T(8,128)(2,1)S(1)}, u32[]{:S(2)}, u32[]{:S(2)}) %collective-permute-start.1) | collective-permute-done | bytes 524320 | tf_op jit(solution)/shard_map/ppermute | solution.py:211
  15.5 0.7 pack.1
  16.2 31.6 %all_to_all.15 = bf16[16,136,128]{2,1,0:T(8,128)(2,1)S(1)} all-to-all(bf16[16,136,128]{2,1,0:T(8,128)(2,1)S(1)} %pack.1), channel_id=1, replica_groups=mesh['q'=2,'p'=2,'z'=8,'x'=4,'h'=2,'c'=2] {'q','z'}, dimensions={0} | all-to-all | bytes 1114112 | tf_op jit(solution)/shard_map/all_to_all | solution.py:219
  47.8 0.1 reduce_sum.12
  47.9 0.1 broadcast_in_dim.4
  48.0 21.1 %all_to_all.16.stat_ref = bf16[16,136,128]{2,1,0:T(8,128)(2,1)S(1)} all-to-all(bf16[16,136,128]{2,1,0:T(8,128)(2,1)S(1)} %broadcast_in_dim.4), channel_id=1, replica_groups=mesh['q'=2,'p'=2,'z'=8,'x'=4,'h'=2,'c'=2] {'q','z'}, dimensions={0} | all-to-all | bytes 1114112 | tf_op jit(solution)/shard_map/all_to_all | solution.py:185
  69.0 3.2 %root.1.mine_ref = bf16[776,512]{1,0:T(8,128)(2,1)S(1)} custom-call(f32[8,128]{1,0:T(8,128)S(1)} %get-tuple-element.7.label_ref, bf16[16,136,128]{2,1,0:T(8,128)(2,1)S(1)} %all_to_all.16.stat_ref), custom_call_target="tpu_custom_call" | custom-call | tf_op jit(solution)/shard_map/root/pallas_call | solution.py:222
  72.3 4.7 %collective-permute-start.2 = (bf16[776,512]{1,0:T(8,128)(2,1)S(1)}, bf16[776,512]{1,0:T(8,128)(2,1)S(1)}, u32[]{:S(2)}, u32[]{:S(2)}) collective-permute-start(bf16[776,512]{1,0:T(8,128)(2,1)S(1)} %root.1.mine_ref), channel_id=1, source_target_pairs={{0,1},{1,0},{2,3},{3,2},{4,5},{5,4},{6,7},{7,6},{8,9},{9,8},{10,11... | collective-permute-start | bytes 2383880 | tf_op jit(solution)/shard_map/ppermute | solution.py:229
  77.0 1.9 %collective-permute-done.2.other_ref = bf16[776,512]{1,0:T(8,128)(2,1)S(1)} collective-permute-done((bf16[776,512]{1,0:T(8,128)(2,1)S(1)}, bf16[776,512]{1,0:T(8,128)(2,1)S(1)}, u32[]{:S(2)}, u32[]{:S(2)}) %collective-permute-start.2) | collective-permute-done | bytes 794656 | tf_op jit(solution)/shard_map/ppermute | solution.py:229
  78.9 0.3 rows.1.rows_ref
  79.2 2.3 %collective-permute-start.3 = (f32[16,512]{1,0:T(8,128)S(1)}, f32[16,512]{1,0:T(8,128)S(1)}, u32[]{:S(2)}, u32[]{:S(2)}) collective-permute-start(f32[16,512]{1,0:T(8,128)S(1)} %rows.1.rows_ref), channel_id=1, source_target_pairs={{1,128},{128,1},{3,130},{130,3},{5,132},{132,5},{7,134},{134,7},{9... | collective-permute-start | bytes 98312 | tf_op jit(solution)/shard_map/ppermute | solution.py:245
  81.5 1.0 %energy.1 = f32[16,1,128]{2,1,0:T(1,128)S(1)} custom-call(f32[8,128]{1,0:T(8,128)S(1)} %get-tuple-element.7.label_ref, bf16[776,512]{1,0:T(8,128)(2,1)S(1)} %root.1.mine_ref, bf16[776,512]{1,0:T(8,128)(2,1)S(1)} %collective-permute-done.2.other_ref), custom_call_target="tpu_custom_call" | custom-call | tf_op jit(solution)/shard_map/energy/pallas_call | solution.py:230
  82.5 13.3 %all_to_all.17.notes_ref = f32[16,1,128]{2,1,0:T(1,128)S(1)} all-to-all(f32[16,1,128]{2,1,0:T(1,128)S(1)} %energy.1), channel_id=1, replica_groups={{0,258,4,262,8,266,12,270,128,386,132,390,136,394,140,398},{256,2,260,6..., dimensions={0} | all-to-all | bytes 16384 | tf_op jit(solution)/shard_map/all_to_all | solution.py:237
  95.8 0.0 collective-permute-done.3.moved_ref
  95.8 0.8 scale.1
Async XLA Ops:
  0.0 11.6 %collective-permute-start = (bf16[512,512]{1,0:T(8,128)(2,1)}, bf16[512,512]{1,0:T(8,128)(2,1)S(1)}, u32[]{:S(2)}, u32[]{:S(2)}) collective-permute-start(bf16[512,512]{1,0:T(8,128)(2,1)} %bitcast.2), channel_id=1, source_target_pairs={{1,128},{128,1},{3,130},{130,3},{5,132},{132,5},{7,134},{134,7},{9... | collective-permute-start | bytes 1572872 | tf_op jit(solution)/shard_map/ppermute | solution.py:202
  11.7 3.8 %collective-permute-start.1 = (bf16[512,512]{1,0:T(8,128)(2,1)S(1)}, bf16[512,512]{1,0:T(8,128)(2,1)S(1)}, u32[]{:S(2)}, u32[]{:S(2)}) collective-permute-start(bf16[512,512]{1,0:T(8,128)(2,1)S(1)} %broadcast_select_fusion.one_ref), channel_id=1, source_target_pairs={{0,1},{1,0},{2,3},{3,2},{4,5},{5,4},{6,7},{7,6},{8,9},{9,8},{10,11... | collective-permute-start | bytes 1572872 | tf_op jit(solution)/shard_map/ppermute | solution.py:211
  72.3 6.6 %collective-permute-start.2 = (bf16[776,512]{1,0:T(8,128)(2,1)S(1)}, bf16[776,512]{1,0:T(8,128)(2,1)S(1)}, u32[]{:S(2)}, u32[]{:S(2)}) collective-permute-start(bf16[776,512]{1,0:T(8,128)(2,1)S(1)} %root.1.mine_ref), channel_id=1, source_target_pairs={{0,1},{1,0},{2,3},{3,2},{4,5},{5,4},{6,7},{7,6},{8,9},{9,8},{10,11... | collective-permute-start | bytes 2383880 | tf_op jit(solution)/shard_map/ppermute | solution.py:229
  79.2 16.6 %collective-permute-start.3 = (f32[16,512]{1,0:T(8,128)S(1)}, f32[16,512]{1,0:T(8,128)S(1)}, u32[]{:S(2)}, u32[]{:S(2)}) collective-permute-start(f32[16,512]{1,0:T(8,128)S(1)} %rows.1.rows_ref), channel_id=1, source_target_pairs={{1,128},{128,1},{3,130},{130,3},{5,132},{132,5},{7,134},{134,7},{9... | collective-permute-start | bytes 98312 | tf_op jit(solution)/shard_map/ppermute | solution.py:245
